TPU v7x, 32 devices: a 4x4x1 block of a 4x4x8 slice. The times are simulated.
32 devices in a mesh: dp: 1 (over z), tx: 4 (over y), ty: 8 (over x, core).
Axes of the slice: x: 4, y: 4, z: 1, core: 2. Of those that a mesh axis runs over, the one named last changes fastest.
The devices are a block of a 4x4x8 slice.
Arguments:
- residual: float32 [1024, 1536], P('dp', 'tx')
- norm_w: float32 [2, 1536], P(None, 'tx')
- w_in: bfloat16 [2, 1536, 2, 3072], P(None, 'tx', None, 'ty')
- conv_w: float32 [2, 3072, 4], P(None, 'ty')
- conv_b: float32 [2, 3072], P(None, 'ty')
- w_x: bfloat16 [2, 3072, 128], P(None, 'ty')
- w_dt: bfloat16 [2, 96, 3072], P(None, None, 'ty')
- dt_bias: float32 [2, 3072], P(None, 'ty')
- a_log: float32 [2, 3072, 16], P(None, 'ty')
- d_skip: float32 [2, 3072], P(None, 'ty')
- w_out: bfloat16 [2, 3072, 1536], P(None, 'ty', 'tx')
- conv_state: bfloat16 [2, 1024, 3072, 3], P(None, ('dp', 'tx'), 'ty')
- ssm_state: float32 [2, 1024, 3072, 16], P(None, ('dp', 'tx'), 'ty')
Outputs:
- output 1: float32 [1024, 1536], P('dp', 'tx')
- output 2: bfloat16 [2, 1024, 3072, 3], P(None, ('dp', 'tx'), 'ty')
- output 3: float32 [2, 1024, 3072, 16], P(None, ('dp', 'tx'), 'ty')
All inputs are finite; a program needn't handle non-finite values.
Results may differ from a plain program's by a relative error of at most 0.0169579.
Values are sent between devices in bfloat16 or wider.
A program may use at most 768 MiB of HBM per device.

v0:
```python
import jax
import jax.numpy as jnp
from jax import lax
from jax.sharding import PartitionSpec as P

NORM_EPS = 1e-5
INNER_EPS = 1e-6


def unit_rms(vec):
    return vec * lax.rsqrt(jnp.mean(vec * vec, axis=-1, keepdims=True) + INNER_EPS)


def channel_update(x_branch, z_branch, conv_prev, ssm_prev, conv_w, conv_b, w_x, w_dt, dt_bias, a_log, d_skip, reduce_fn):
    n_rank = w_dt.shape[0]
    n_state = a_log.shape[-1]
    window = jnp.concatenate([conv_prev, x_branch[:, :, None]], axis=-1)
    conv_val = jnp.sum(window.astype(jnp.float32) * conv_w, axis=-1) + conv_b
    x_conv = jax.nn.silu(conv_val).astype(jnp.bfloat16)
    x_dbl = reduce_fn(jnp.dot(x_conv, w_x, preferred_element_type=jnp.float32))
    dt_low = unit_rms(x_dbl[:, :n_rank])
    b_mat = unit_rms(x_dbl[:, n_rank:n_rank + n_state])
    c_mat = unit_rms(x_dbl[:, n_rank + n_state:])
    delta = jax.nn.softplus(jnp.dot(dt_low.astype(jnp.bfloat16), w_dt, preferred_element_type=jnp.float32) + dt_bias)
    x_float = x_conv.astype(jnp.float32)
    decay = jnp.exp(delta[:, :, None] * -jnp.exp(a_log))
    ssm_new = decay * ssm_prev + (delta * x_float)[:, :, None] * b_mat[:, None, :]
    state_val = jnp.sum(ssm_new * c_mat[:, None, :], axis=-1)
    gated = ((state_val + d_skip * x_float) * jax.nn.silu(z_branch.astype(jnp.float32))).astype(jnp.bfloat16)
    return gated, window[:, :, 1:], ssm_new


def solution(mesh):
    n_dmod = mesh.shape["tx"]

    def sum_over_ty(part_sum):
        return lax.psum(part_sum.astype(jnp.bfloat16), "ty").astype(jnp.float32)

    def local_step(residual, norm_w, w_in, conv_w, conv_b, w_x, w_dt, dt_bias, a_log, d_skip, w_out, conv_state, ssm_state):
        d_model = residual.shape[1] * n_dmod
        conv_list = []
        ssm_list = []
        for layer_idx in range(norm_w.shape[0]):
            sq_part = jnp.sum(residual * residual, axis=-1, keepdims=True)
            sq_total = lax.psum(sq_part, "tx")
            normed = (residual * lax.rsqrt(sq_total / d_model + NORM_EPS) * norm_w[layer_idx]).astype(jnp.bfloat16)
            proj_part = jnp.einsum("bd,dke->bke", normed, w_in[layer_idx], preferred_element_type=jnp.float32)
            proj_in = lax.psum_scatter(proj_part.astype(jnp.bfloat16), "tx", scatter_dimension=0, tiled=True)
            gated, conv_new, ssm_new = channel_update(proj_in[:, 0, :], proj_in[:, 1, :], conv_state[layer_idx], ssm_state[layer_idx], conv_w[layer_idx], conv_b[layer_idx], w_x[layer_idx], w_dt[layer_idx], dt_bias[layer_idx], a_log[layer_idx], d_skip[layer_idx], sum_over_ty)
            gated_rows = lax.all_gather(gated, "tx", axis=0, tiled=True)
            out_part = jnp.dot(gated_rows, w_out[layer_idx], preferred_element_type=jnp.float32)
            residual = residual + sum_over_ty(out_part)
            conv_list.append(conv_new)
            ssm_list.append(ssm_new)
        return residual, jnp.stack(conv_list), jnp.stack(ssm_list)

    cache_spec = P(None, ("dp", "tx"), "ty", None)
    in_specs = (P("dp", "tx"), P(None, "tx"), P(None, "tx", None, "ty"), P(None, "ty", None), P(None, "ty"), P(None, "ty", None), P(None, None, "ty"), P(None, "ty"), P(None, "ty", None), P(None, "ty"), P(None, "ty", "tx"), cache_spec, cache_spec)
    out_specs = (P("dp", "tx"), cache_spec, cache_spec)
    return jax.shard_map(local_step, mesh=mesh, in_specs=in_specs, out_specs=out_specs, check_vma=False)
```

profile of v0, /device:TPU:97, one launch (start us, length us, event | category | flops | bytes accessed | tf_op | source)
XLA Modules:
  0.0 383.4 jit_solution(8638184159036011989)
XLA Ops:
  7.3 1.6 multiply_reduce_fusion.3
  8.9 11.4 %psum.42 = f32[1024,1]{0,1:T(1,128)S(1)} all-reduce(f32[1024,1]{0,1:T(1,128)S(1)} %bitcast.91), channel_id=1, replica_groups=mesh['dp'=1,'tx'=4,'ty'=8] {'tx'}, use_global_device_ids=true, to_apply=%region_1.0 | all-reduce | flops 1024 | bytes 8192 | tf_op jit(solution)/shard_map/psum | solution.py:45
  20.3 0.8 slice_reduce_fusion.7
  21.1 2.9 fusion.44
  24.0 3.6 convolution_convert_fusion.1
  27.8 0.6 slice_reduce_fusion.1
  28.4 0.6 negate_bitcast_fusion
  29.0 1.4 slice_bitcast_fusion
  30.4 21.4 %reduce-scatter.3.cloned.1.call-done = bf16[256,2,384]{2,0,1:T(8,128)(2,1)} async-done(((bf16[1024,2,384]{2,0,1:T(8,128)(2,1)}), bf16[256,2,384]{2,0,1:T(8,128)(2,1)}) %reduce-scatter.3.cloned.1.call-update) | async-done | bytes 393232 | tf_op jit(solution)/shard_map/reduce_scatter | solution.py:48
  51.8 0.9 slice_bitcast_fusion.5
  52.8 0.2 multiply_reduce_fusion.2
  52.9 0.1 multiply_convert_fusion.3
  53.1 0.8 convolution_convert_fusion.5
  54.0 53.3 %all-reduce.5.cloned.1.call-done = bf16[256,128]{1,0:T(8,128)(2,1)} async-done(((bf16[256,128]{1,0:T(8,128)(2,1)}), bf16[256,128]{1,0:T(8,128)(2,1)}) %all-reduce.5.cloned.1.call-update) | async-done | bytes 65552 | tf_op jit(solution)/shard_map/psum | solution.py:37
  107.3 0.8 convert_element_type.83
  108.2 0.1 multiply_reduce_fusion.9
  108.3 0.3 multiply_reduce_fusion.8
  108.6 0.2 slice_multiply_fusion.3
  108.8 0.4 convert_multiply_fusion.5
  109.3 6.3 %fusion.5 = f32[256,384]{1,0:T(8,128)S(1)} fusion(f32[2,256,384,16]{2,3,1,0:T(8,128)} %param.25, f32[256,16]{1,0:T(8,128)S(1)} %get-tuple-element.24, f32[256,16]{1,0:T(8,128)S(1)} %get-tuple-element.23, f32[256,384]{1,0:T(8,128)S(1)} %get-tuple-element.29, f32[384,16]{0,1:T(8,128)S(1)} %get-tuple-element.26, f32[256,384]{1,0:T(8,128)S(1)} %get-tuple-element.30), kind=kLoop, calls=%fused_computation.8 | loop fusion | flops 9338880 | bytes 7528448 | tf_op jit(solution)/shard_map/reduce_sum | solution.py:28
  115.7 1.2 fusion.20
  116.8 11.2 %all_gather.6 = bf16[1024,384]{1,0:T(8,128)(2,1)S(1)} all-gather(bf16[256,384]{1,0:T(8,128)(2,1)S(1)} %fusion.20), channel_id=1, replica_groups=mesh['dp'=1,'tx'=4,'ty'=8] {'tx'}, dimensions={0}, use_global_device_ids=true | all-gather | bytes 983040 | tf_op jit(solution)/shard_map/all_gather | solution.py:50
  128.0 2.5 convolution_convert_fusion.3
  130.7 58.8 %all-reduce.7.cloned.1.call-done = bf16[1024,384]{1,0:T(8,128)(2,1)} async-done(((bf16[1024,384]{1,0:T(8,128)(2,1)}), bf16[1024,384]{1,0:T(8,128)(2,1)}) %all-reduce.7.cloned.1.call-update) | async-done | bytes 786448 | tf_op jit(solution)/shard_map/psum | solution.py:37
  189.4 1.4 multiply_reduce_fusion.1
  190.8 8.5 %psum.45 = f32[1024,1]{0,1:T(1,128)S(1)} all-reduce(f32[1024,1]{0,1:T(1,128)S(1)} %bitcast.92), channel_id=1, replica_groups=mesh['dp'=1,'tx'=4,'ty'=8] {'tx'}, use_global_device_ids=true, to_apply=%region_11.12 | all-reduce | flops 1024 | bytes 8192 | tf_op jit(solution)/shard_map/psum | solution.py:45
  199.4 3.5 convolution_convert_fusion
  203.1 23.5 %reduce-scatter.5.cloned.1.call-done = bf16[256,2,384]{2,0,1:T(8,128)(2,1)} async-done(((bf16[1024,2,384]{2,0,1:T(8,128)(2,1)}), bf16[256,2,384]{2,0,1:T(8,128)(2,1)}) %reduce-scatter.5.cloned.1.call-update) | async-done | bytes 393232 | tf_op jit(solution)/shard_map/reduce_scatter | solution.py:48
  226.5 0.9 slice_bitcast_fusion.3
  227.5 0.9 fusion.15
  228.4 0.2 multiply_reduce_fusion
  228.5 0.1 multiply_convert_fusion.2
  228.6 1.7 convolution_convert_fusion.4
  230.4 0.2 all-reduce.11.cloned.1.call-start
  230.7 2.2 pad_maximum_fusion.1
  232.9 50.4 %all-reduce.9.cloned.1.call-done = bf16[256,128]{1,0:T(8,128)(2,1)} async-done(((bf16[256,128]{1,0:T(8,128)(2,1)}), bf16[256,128]{1,0:T(8,128)(2,1)}) %all-reduce.9.cloned.1.call-update) | async-done | bytes 65552 | tf_op jit(solution)/shard_map/psum | solution.py:37
  283.3 0.8 convert_element_type.96
  284.2 0.3 multiply_reduce_fusion.5
  284.5 0.2 slice_multiply_fusion.1
  284.7 1.5 convert_multiply_fusion.3
  286.3 13.3 %multiply_add_fusion.1 = (f32[1,256,384,16]{2,3,1,0:T(8,128)}, f32[1,256,384,16]{2,3,1,0:T(8,128)}) fusion(f32[2,256,384,16]{2,3,1,0:T(8,128)} %param.25, f32[256,16]{1,0:T(8,128)} %copy-done.4, f32[256,384]{1,0:T(8,128)} %copy-done.2, f32[384,16]{0,1:T(8,128)} %copy-done.8, f32[256,384]{1,0:T(8,128)} %copy-done.3, f32[256,16]{1,0:T(8,128)S(1)} %get-tuple-element.21, ...), kind=kLoop, calls=%fused_computation.10 | loop fusion | flops 12582912 | bytes 26820608 | tf_op jit(solution)/shard_map/add | solution.py:27
  299.7 2.5 fusion.2
  302.2 0.2 fusion.23
  302.4 11.2 %all_gather.7 = bf16[1024,384]{1,0:T(8,128)(2,1)S(1)} all-gather(bf16[256,384]{1,0:T(8,128)(2,1)S(1)} %fusion.23), channel_id=1, replica_groups=mesh['dp'=1,'tx'=4,'ty'=8] {'tx'}, dimensions={0}, use_global_device_ids=true | all-gather | bytes 983040 | tf_op jit(solution)/shard_map/all_gather | solution.py:50
  313.6 1.5 convolution_convert_fusion.2
  315.2 10.3 %pad_maximum_fusion = f32[2,256,384,16]{2,3,1,0:T(8,128)} fusion(f32[1,256,384,16]{2,3,1,0:T(8,128)} %get-tuple-element.16, f32[1,256,384,16]{2,3,1,0:T(8,128)} %get-tuple-element.15), kind=kLoop, calls=%fused_computation | loop fusion | flops 3145728 | bytes 25165824 | tf_op jit(solution)/shard_map/stack | solution.py:55
  325.5 48.5 %all-reduce.11.cloned.1.call-done = bf16[1024,384]{1,0:T(8,128)(2,1)} async-done(((bf16[1024,384]{1,0:T(8,128)(2,1)}), bf16[1024,384]{1,0:T(8,128)(2,1)}) %all-reduce.11.cloned.1.call-update) | async-done | bytes 786448 | tf_op jit(solution)/shard_map/psum | solution.py:37
  374.0 2.5 convert_add_fusion
  (62 shorter events, 1.0 us)
Async XLA Ops:
  7.2 20.5 %copy-start.12 = (f32[2,384]{1,0:T(2,128)S(1)}, f32[2,384]{1,0:T(2,128)}, u32[]{:S(2)}) copy-start(f32[2,384]{1,0:T(2,128)} %param.17) | copy-start | bytes 9220
  7.2 20.6 %copy-start.13 = (f32[2,384]{1,0:T(2,128)S(1)}, f32[2,384]{1,0:T(2,128)}, u32[]{:S(2)}) copy-start(f32[2,384]{1,0:T(2,128)} %param.20) | copy-start | bytes 9220
  7.2 21.2 %copy-start.11 = (f32[2,384,4]{1,2,0:T(4,128)S(1)}, f32[2,384,4]{1,2,0:T(4,128)}, u32[]{:S(2)}) copy-start(f32[2,384,4]{1,2,0:T(4,128)} %param.16) | copy-start | bytes 36868
  7.2 21.2 %copy-start.10 = (f32[2,384,16]{1,2,0:T(8,128)S(1)}, f32[2,384,16]{1,2,0:T(8,128)}, u32[]{:S(2)}) copy-start(f32[2,384,16]{1,2,0:T(8,128)} %param.21) | copy-start | bytes 147460
  7.2 44.6 %reduce-scatter.3.cloned.1.call-start = ((), (), s32[]{:S(2)}) async-start(), calls=%async_computation.2 | async-start | bytes 1966080 | tf_op jit(solution)/shard_map/reduce_scatter | solution.py:48
  8.9 44.1 %copy-start.9 = (bf16[2,384,128]{2,1,0:T(8,128)(2,1)S(1)}, bf16[2,384,128]{2,1,0:T(8,128)(2,1)}, u32[]{:S(2)}) copy-start(bf16[2,384,128]{2,1,0:T(8,128)(2,1)} %param.18) | copy-start | bytes 589828
  21.1 32.9 %copy-start.14 = (f32[2,384]{1,0:T(2,128)S(1)}, f32[2,384]{1,0:T(2,128)}, u32[]{:S(2)}) copy-start(f32[2,384]{1,0:T(2,128)} %param.22) | copy-start | bytes 9220
  24.0 84.8 %copy-start.15 = (bf16[2,96,384]{2,1,0:T(8,128)(2,1)S(1)}, bf16[2,96,384]{2,1,0:T(8,128)(2,1)}, u32[]{:S(2)}) copy-start(bf16[2,96,384]{2,1,0:T(8,128)(2,1)} %param.19) | copy-start | bytes 442372
  27.6 79.7 %all-reduce.5.cloned.1.call-start = ((), (), s32[]{:S(2)}) async-start(), calls=%async_computation.3 | async-start | bytes 131072 | tf_op jit(solution)/shard_map/psum | solution.py:37
  29.0 86.7 %copy-start.8 = (f32[384,16]{0,1:T(8,128)}, f32[384,16]{0,1:T(8,128)S(1)}, u32[]{:S(2)}) copy-start(f32[384,16]{0,1:T(8,128)S(1)} %get-tuple-element.26) | copy-start | bytes 73732
  53.9 135.5 %all-reduce.7.cloned.1.call-start = ((), (), s32[]{:S(2)}) async-start(), calls=%async_computation.4 | async-start | bytes 1572864 | tf_op jit(solution)/shard_map/psum | solution.py:37
  108.8 21.7 %copy-start.4 = (f32[256,16]{1,0:T(8,128)}, f32[256,16]{1,0:T(8,128)S(1)}, u32[]{:S(2)}) copy-start(f32[256,16]{1,0:T(8,128)S(1)} %get-tuple-element.23) | copy-start | bytes 49156
  109.3 7.6 %copy-start.2 = (f32[256,384]{1,0:T(8,128)}, f32[256,384]{1,0:T(8,128)S(1)}, u32[]{:S(2)}) copy-start(f32[256,384]{1,0:T(8,128)S(1)} %get-tuple-element.29) | copy-start | bytes 1179652
  109.3 18.8 %copy-start.3 = (f32[256,384]{1,0:T(8,128)}, f32[256,384]{1,0:T(8,128)S(1)}, u32[]{:S(2)}) copy-start(f32[256,384]{1,0:T(8,128)S(1)} %get-tuple-element.30) | copy-start | bytes 1179652
  109.3 80.2 %copy-start = (f32[1024,384]{1,0:T(8,128)S(1)}, f32[1024,384]{1,0:T(8,128)}, u32[]{:S(2)}) copy-start(f32[1024,384]{1,0:T(8,128)} %param.13) | copy-start | bytes 4718596
  130.6 95.9 %reduce-scatter.5.cloned.1.call-start = ((), (), s32[]{:S(2)}) async-start(), calls=%async_computation.5 | async-start | bytes 1966080 | tf_op jit(solution)/shard_map/reduce_scatter | solution.py:48
  202.9 80.3 %all-reduce.9.cloned.1.call-start = ((), (), s32[]{:S(2)}) async-start(), calls=%async_computation.6 | async-start | bytes 131072 | tf_op jit(solution)/shard_map/psum | solution.py:37
  230.4 143.6 %all-reduce.11.cloned.1.call-start = ((), (), s32[]{:S(2)}) async-start(), calls=%async_computation.7 | async-start | bytes 1572864 | tf_op jit(solution)/shard_map/psum | solution.py:37
  284.7 14.9 %slice-start = ((s8[12582912]{0:T(1024)(128)(4,1)}), s8[4194304]{0:T(1024)(128)(4,1)S(1)}, s32[]{:S(2)}) async-start(s8[12582912]{0:T(1024)(128)(4,1)} %bitcast.88), calls=%async_computation.8 | async-start | bytes 8388608
  286.2 13.4 %slice-start.1 = ((s8[12582912]{0:T(1024)(128)(4,1)}), s8[4194304]{0:T(1024)(128)(4,1)S(1)}, s32[]{:S(2)}) async-start(s8[12582912]{0:T(1024)(128)(4,1)} %bitcast.88), calls=%async_computation.9 | async-start | bytes 8388608
  286.2 13.4 %slice-start.2 = ((s8[12582912]{0:T(1024)(128)(4,1)}), s8[4194304]{0:T(1024)(128)(4,1)S(1)}, s32[]{:S(2)}) async-start(s8[12582912]{0:T(1024)(128)(4,1)} %bitcast.88), calls=%async_computation.10 | async-start | bytes 8388608
  286.3 13.4 %copy-start.7 = (f32[384,16]{0,1:T(8,128)S(1)}, f32[384,16]{0,1:T(8,128)}, u32[]{:S(2)}) copy-start(f32[384,16]{0,1:T(8,128)} %get-tuple-element.25) | copy-start | bytes 73732
  299.6 2.6 copy-start.6
  299.6 14.0 %copy-start.5 = (bf16[2,384,384]{2,1,0:T(8,128)(2,1)S(1)}, bf16[2,384,384]{2,1,0:T(8,128)(2,1)}, u32[]{:S(2)}) copy-start(bf16[2,384,384]{2,1,0:T(8,128)(2,1)} %param.23) | copy-start | bytes 1769476
  315.2 58.8 %copy-start.1 = (bf16[1024,384]{1,0:T(8,128)(2,1)S(1)}, bf16[1024,384]{1,0:T(8,128)(2,1)}, u32[]{:S(2)}) copy-start(bf16[1024,384]{1,0:T(8,128)(2,1)} %all-reduce.7.cloned.1.call-done) | copy-start | bytes 2359300
Sparse Core Ops, SparseCore 0:
  27.8 23.9 reduce-scatter.2
  54.7 52.5 all-reduce.4
  130.7 58.6 all-reduce.6
  203.0 23.4 reduce-scatter.4
  230.5 52.6 all-reduce.8
  315.3 58.6 all-reduce.10
where the time goes:
time: 385 us; the launch traced here: 383 us
  waiting for transfers between devices  256 us (66%)
  other arithmetic  46.6 us (12%)
  blocking collectives  42.3 us (11%)
  matrix products  15.6 us (4%)
  between operations  14.5 us (4%)
  local copies, waits for them, and re-layouts  7.65 us (2%)
    psum x4, waiting for transfers between devices, sum_over_ty(): return lax.psum(part_sum.astype(jnp.bfloat16), 'ty').astype(jnp.float32)  211 us
    reduce_scatter x2, waiting for transfers between devices, local_step(): lax.psum_scatter(proj_part.astype(jnp.bfloat16), 'tx', scatter_dimension=...  44.9 us
    all_gather x2, blocking collectives, local_step(): gated_rows = lax.all_gather(gated, 'tx', axis=0, tiled=True)  22.4 us
    psum x2, blocking collectives, local_step(): sq_total = lax.psum(sq_part, 'tx')  19.9 us
    another operation x4, other arithmetic, local_step(): return (residual, jnp.stack(conv_list), jnp.stack(ssm_list))  13.4 us
    add x1, other arithmetic, channel_update(): decay * ssm_prev + (delta * x_float)[:, :, None] * b_mat[:, None, :]  13.3 us
    reduce_sum x2, other arithmetic, channel_update(): state_val = jnp.sum(ssm_new * c_mat[:, None, :], axis=-1)  8.85 us
  transfers between devices with their start and end apart: 6, of which 6 were waited for; matrix products, arithmetic and copies ran while one was open for 4% of the time, Pallas kernels for 0%

commit v1 on v0

v1 whole, which is shorter than its diff:
```python
import functools

import jax
import jax.numpy as jnp
from jax import lax
from jax.experimental import pallas as pl
from jax.experimental.pallas import tpu as pltpu
from jax.sharding import PartitionSpec as P

NORM_EPS = 1e-5
INNER_EPS = 1e-6
MESH = pl.DeviceIdType.MESH
F32 = jnp.float32
BF16 = jnp.bfloat16


def silu(v):
    return v * jax.nn.sigmoid(v)


def softplus(v):
    return jnp.maximum(v, 0.0) + jnp.log1p(jnp.exp(-jnp.abs(v)))


def loop(n, body):
    def step(i, carry):
        body(i)
        return carry

    lax.fori_loop(0, n, step, 0)


def mixer_kernel(names, nt, nj, n_state, *refs):
    R = dict(zip(names, refs))
    r0, nw, conv_w, conv_b = R["r0"], R["nw"], R["conv_w"], R["conv_b"]
    dt_bias, d_skip, a_log = R["dt_bias"], R["d_skip"], R["a_log"]
    rows_all, dm = r0.shape
    ch = a_log.shape[-1]
    rt = rows_all // nt
    half = rt // 2
    rj = rt // nj
    n_rank = R["px"].shape[-1] - 2 * n_state
    d_model = dm * nt

    t = lax.axis_index("tx")
    j = lax.axis_index("ty")
    tr, to, tl = lax.rem(t + 1, nt), lax.rem(t + 2, nt), lax.rem(t + 3, nt)
    core = lax.rem(j, 2)
    jp = j + 1 - 2 * core
    jr, jo, jl = lax.rem(j + 2, nj), lax.rem(j + 4, nj), lax.rem(j + 6, nj)
    x, xr, xo, xl = j // 2, jr // 2, jo // 2, jl // 2

    count = {"r": 0, "l": 0}
    sent = []

    def send(src, dst, **dev):
        i = count["r"]
        count["r"] += 1
        cp = pltpu.make_async_remote_copy(
            src_ref=src, dst_ref=dst, send_sem=R["send_sem"].at[i], recv_sem=R["recv_sem"].at[i],
            device_id=dev, device_id_type=MESH)
        cp.start()
        sent.append(cp)
        return cp

    def local(src, dst):
        i = count["l"]
        count["l"] += 1
        cp = pltpu.make_async_copy(src, dst, R["loc_sem"].at[i])
        cp.start()
        return cp

    ld_win0 = local(R["w_in"].at[0], R["w0"])
    ld_conv = local(R["conv_state"], R["convs"])
    ld_wx = local(R["w_x"], R["wx"])
    ld_wdt = local(R["w_dt"], R["wdt"])
    ld_wo = [local(R["w_out"].at[l], R["wo_g"].at[l, t]) for l in range(2)]
    ld_wi1 = [local(R["w_in"].at[1, k], R["wi_g"].at[k, t]) for k in range(2)]
    ld_ssm = [local(R["ssm"].at[l], R["st"].at[l]) for l in range(2)]

    barrier = pltpu.get_barrier_semaphore()
    for peer in (tr, to, tl):
        pl.semaphore_signal(barrier, inc=1, device_id={"tx": peer}, device_id_type=MESH)
    for peer in (jp, jr, jo, jl):
        pl.semaphore_signal(barrier, inc=1, device_id={"ty": peer}, device_id_type=MESH)

    def stat_body(b):
        rows = pl.ds(pl.multiple_of(b * 128, 128), 128)
        r = r0[rows, :]
        sq = r * r
        part = sq[:, :128]
        for i in range(1, dm // 128):
            part = part + sq[:, i * 128:(i + 1) * 128]
        R["stat"][pl.ds(b, 1), :] = jnp.sum(part.T, axis=0, keepdims=True)
        col = jnp.sum(part, axis=1, keepdims=True)
        lr = lax.rsqrt(col / dm + NORM_EPS)
        R["h0"][rows, :] = (r * lr * nw[0:1, :]).astype(BF16)

    loop(rows_all // 128, stat_body)
    pl.semaphore_wait(barrier, 7)
    stats = [send(R["stat"], R["stat_rx"].at[i], tx=p) for i, p in enumerate((tr, to, tl))]

    ld_win0.wait()
    pf, stg = R["pf"], R["stg"]

    def mm_body(b):
        rows = pl.ds(pl.multiple_of(b * 128, 128), 128)
        for k in range(2):
            pf[k, rows, :] = jnp.dot(R["h0"][rows, :], R["w0"][k], preferred_element_type=F32)

    loop(rows_all // 128, mm_body)
    for s in stats:
        s.wait_recv()

    def fac_body(b):
        rows = pl.ds(pl.multiple_of(b * 128, 128), 128)
        own = R["stat"][pl.ds(b, 1), :]
        tot = own
        for i in range(nt - 1):
            tot = tot + R["stat_rx"][i, pl.ds(b, 1), :]
        f = lax.rsqrt(tot / d_model + NORM_EPS) * jnp.sqrt(own / dm + NORM_EPS)
        fac = jnp.broadcast_to(f, (128, 128)).T
        R["fac"][rows, :] = fac
        for i in range(ch // 128):
            cols = slice(i * 128, (i + 1) * 128)
            v = pf[0, rows, cols] * fac
            pf[0, rows, cols] = v
            stg[0, rows, cols] = v.astype(BF16)

    loop(rows_all // 128, fac_body)
    rx, tx2 = R["rx"], R["tx2"]

    def part_rows(owner, h):
        return pl.ds(pl.multiple_of(owner * rt + h * half, half), half)

    def rs_first(k):
        return (send(stg.at[k, part_rows(to, 0)], rx.at[k, 0], tx=tr),
                send(stg.at[k, part_rows(to, 1)], rx.at[k, 1], tx=tl),
                send(stg.at[k, part_rows(tl, 0)], rx.at[k, 2], tx=tl),
                send(stg.at[k, part_rows(tr, 1)], rx.at[k, 3], tx=tr))

    def rs_second(k, first):
        first[0].wait_recv()
        tx2[k, 0] = (rx[k, 0].astype(F32) + pf[k, part_rows(tr, 0), :]).astype(BF16)
        a = send(tx2.at[k, 0], rx.at[k, 4], tx=tr)
        first[1].wait_recv()
        tx2[k, 1] = (rx[k, 1].astype(F32) + pf[k, part_rows(tl, 1), :]).astype(BF16)
        b = send(tx2.at[k, 1], rx.at[k, 5], tx=tl)
        return a, b

    def rs_last(k, first, second, out):
        for cp in (first[2], first[3], *second):
            cp.wait_recv()
        for h in range(2):
            v = pf[k, part_rows(t, h), :] + rx[k, 2 + h].astype(F32) + rx[k, 4 + h].astype(F32)
            out[h * half:(h + 1) * half, :] = v.astype(BF16)

    x_first = rs_first(0)

    def z_body(b):
        rows = pl.ds(pl.multiple_of(b * 128, 128), 128)
        fac = R["fac"][rows, :]
        for i in range(ch // 128):
            cols = slice(i * 128, (i + 1) * 128)
            v = pf[1, rows, cols] * fac
            pf[1, rows, cols] = v
            stg[1, rows, cols] = v.astype(BF16)

    loop(rows_all // 128, z_body)
    x_second = rs_second(0, x_first)
    z_first = rs_first(1)
    nw1 = R["nw1_g"]
    nw1[t] = nw[1:2, :]
    nw_cp = [send(nw1.at[t], nw1.at[t], tx=p) for p in (tr, to, tl)]
    r0g = R["r0g"]
    r0_cp = []
    for p in (tr, to, tl):
        src = r0.at[pl.ds(pl.multiple_of(p * rt + j * rj, rj), rj)]
        r0_cp.append(send(src, r0g.at[t], tx=p))
    r0g[t] = r0[pl.ds(pl.multiple_of(t * rt + j * rj, rj), rj), :]

    class Gather:
        def __init__(self, buf):
            self.buf, self.half = buf, buf.shape[1] // 2

        def own(self):
            self.a = send(self.buf.at[t], self.buf.at[t], tx=tr)
            self.b = send(self.buf.at[t], self.buf.at[t], tx=tl)

        def relay(self):
            self.a.wait_recv()
            lo, hi = pl.ds(0, self.half), pl.ds(self.half, self.half)
            self.c = send(self.buf.at[tl, lo], self.buf.at[tl, lo], tx=tr)
            self.b.wait_recv()
            self.d = send(self.buf.at[tr, hi], self.buf.at[tr, hi], tx=tl)

        def done(self):
            self.c.wait_recv()
            self.d.wait_recv()

    wo = [Gather(R["wo_g"].at[l]) for l in range(2)]
    wi = [Gather(R["wi_g"].at[k]) for k in range(2)]
    xib, zb, xcf, xcb = R["xib"], R["zb"], R["xcf"], R["xcb"]
    outs = []

    def conv_proj(l):
        def body(b):
            rows = pl.ds(pl.multiple_of(b * 32, 32), 32)
            v = xib[l, rows, :].astype(F32) * conv_w[l, 3:4, :]
            for i in range(3):
                v = v + R["convs"][l, i, rows, :].astype(F32) * conv_w[l, i:i + 1, :]
            xc = silu(v + conv_b[l:l + 1, :]).astype(BF16)
            xcb[l, rows, :] = xc
            xcf[rows, :] = xc.astype(F32)

        loop(rt // 32, body)
        p = jnp.dot(xcb[l], R["wx"][l], preferred_element_type=F32)
        R["px"][...] = p
        R["pst"][l] = p.astype(BF16)
        outs.append(local(xib.at[l], R["xi_out"].at[l]))
        outs.append(local(xcb.at[l], R["xc_out"].at[l]))

    def half_rows(c):
        return pl.ds(pl.multiple_of(c * half, half), half)

    def p_pair(l):
        return send(R["pst"].at[l, half_rows(1 - core)], R["pr0"].at[l], ty=jp)

    def p_cross(l, cp):
        cp.wait_recv()
        q = R["px"][half_rows(core), :] + R["pr0"][l].astype(F32)
        R["px"][half_rows(core), :] = q
        R["qs"][l] = q.astype(BF16)
        return [send(R["qs"].at[l], R["pr1"].at[l, i], ty=p) for i, p in enumerate((jr, jo, jl))]

    def p_finish(l, cps):
        for cp in cps:
            cp.wait_recv()
        q = R["px"][half_rows(core), :]
        for i in range(3):
            q = q + R["pr1"][l, i].astype(F32)
        R["px"][half_rows(core), :] = q
        R["tot"][l] = q.astype(BF16)
        cp = send(R["tot"].at[l], R["pr2"].at[l], ty=jp)
        cp.wait_recv()
        R["px"][half_rows(1 - core), :] = R["pr2"][l].astype(F32)

    def deltas(l):
        for h in range(2):
            rows = slice(h * half, (h + 1) * half)
            p = R["px"][rows, :]
            lane = lax.broadcasted_iota(jnp.int32, p.shape, 1)
            is_dt = lane < n_rank
            is_b = jnp.logical_and(lane >= n_rank, lane < n_rank + n_state)
            sq = p * p

            def scale_of(mask, n):
                tot = jnp.sum(jnp.where(mask, sq, 0.0), axis=1, keepdims=True)
                return lax.rsqrt(tot / n + INNER_EPS)

            s_dt = scale_of(is_dt, n_rank)
            s_b = scale_of(is_b, n_state)
            s_c = scale_of(lane >= n_rank + n_state, n_state)
            pn = p * jnp.where(is_dt, s_dt, jnp.where(is_b, s_b, s_c))
            low = jnp.where(is_dt, pn, 0.0).astype(BF16)
            raw = jnp.dot(low, R["wdt"][l], preferred_element_type=F32) + dt_bias[l:l + 1, :]
            R["dtb"][l, rows, :] = softplus(raw)
            bc = pn.T[n_rank:, :]
            for g in range(half // 8):
                R["btg"][l, h * (half // 8) + g] = pltpu.roll(bc, (half - 8 * g) % half, 1)
        outs.append(local(R["dtb"].at[l], R["dt_out"].at[l]))
        outs.append(local(R["btg"].at[l], R["bt_out"].at[l]))

    def scan_step(l):
        neg_a = -jnp.exp(a_log[l])
        skip = d_skip[l:l + 1, :]

        def body(g):
            rows = pl.ds(pl.multiple_of(g * 8, 8), 8)
            bt = R["btg"][l, g]
            dt8 = R["dtb"][l, rows, :]
            xc8 = xcf[rows, :]
            dx8 = dt8 * xc8
            ys = []
            for b in range(8):
                s = R["st"][l, g * 8 + b]
                b_col = jnp.broadcast_to(bt[:n_state, b:b + 1], s.shape)
                c_col = jnp.broadcast_to(bt[n_state:, b:b + 1], s.shape)
                s = jnp.exp(dt8[b:b + 1, :] * neg_a) * s + dx8[b:b + 1, :] * b_col
                ys.append(jnp.sum(s * c_col, axis=0, keepdims=True))
            R["ys"][rows, :] = jnp.concatenate(ys, axis=0) + skip * xc8

        loop(rt // 8, body)

    def gate():
        def body(b):
            rows = pl.ds(pl.multiple_of(b * 32, 32), 32)
            R["yb"][rows, :] = (R["ys"][rows, :] * silu(zb[rows, :].astype(F32))).astype(BF16)

        loop(rt // 32, body)

    of, ost, css, sums = R["of"], R["ost"], R["css"], R["sums"]

    def out_proj(l):
        for i in range(nt):
            o = jnp.dot(R["yb"][...], R["wo_g"][l, i], preferred_element_type=F32)
            for q in range(nj):
                v = o[q * rj:(q + 1) * rj, :]
                of[q, i] = v
                ost[l, q % 2, q // 2, i] = v.astype(BF16)
        return send(ost.at[l, 1 - core], R["opr"].at[l], ty=jp)

    def out_sums(l, cp):
        cp.wait_recv()

        def body(q):
            v = of[2 * q + core] + R["opr"][l, q].astype(F32)
            sums[q] = v
            css[l, q] = v.astype(BF16)

        loop(nj // 2, body)

    lo, hi = pl.ds(0, nt // 2), pl.ds(nt // 2, nt // 2)

    def out_reduce(l):
        ra, rb = R["rxs"], R["tx2s"]
        c0 = send(css.at[l, xo, lo], ra.at[l, 0], ty=jr)
        c1 = send(css.at[l, xo, hi], ra.at[l, 1], ty=jl)
        c2 = send(css.at[l, xl, lo], ra.at[l, 2], ty=jl)
        c3 = send(css.at[l, xr, hi], ra.at[l, 3], ty=jr)
        c0.wait_recv()
        rb[l, 0] = (ra[l, 0].astype(F32) + sums[xr, lo]).astype(BF16)
        c4 = send(rb.at[l, 0], ra.at[l, 4], ty=jr)
        c1.wait_recv()
        rb[l, 1] = (ra[l, 1].astype(F32) + sums[xl, hi]).astype(BF16)
        c5 = send(rb.at[l, 1], ra.at[l, 5], ty=jl)
        for cp in (c2, c3, c4, c5):
            cp.wait_recv()
        d = R["delta"]
        for h, part in enumerate((lo, hi)):
            v = sums[x, part] + ra[l, 2 + h].astype(F32) + ra[l, 4 + h].astype(F32)
            if l:
                v = v + d[part]
            d[part] = v

    def gather_ty(buf, between=None):
        a = send(buf.at[j], buf.at[j], ty=jr)
        b = send(buf.at[j], buf.at[j], ty=jl)
        waits = [send(buf.at[j], buf.at[j], ty=jp)]
        if between is not None:
            between()
        a.wait_recv()
        c = send(buf.at[jl, lo], buf.at[jl, lo], ty=jr)
        waits.append(send(buf.at[jl], buf.at[jl], ty=jp))
        b.wait_recv()
        d = send(buf.at[jr, hi], buf.at[jr, hi], ty=jl)
        waits.append(send(buf.at[jr], buf.at[jr], ty=jp))
        c.wait_recv()
        waits.append(send(buf.at[jo, lo], buf.at[jo, lo], ty=jp))
        d.wait_recv()
        waits.append(send(buf.at[jo, hi], buf.at[jo, hi], ty=jp))
        for cp in waits:
            cp.wait_recv()

    ld_conv.wait()
    ld_wx.wait()
    rs_last(0, x_first, x_second, xib.at[0])
    conv_proj(0)
    cp = p_pair(0)
    cps = p_cross(0, cp)
    z_second = rs_second(1, z_first)
    for cp in ld_wo:
        cp.wait()
    wo[0].own()
    ld_wdt.wait()
    p_finish(0, cps)
    deltas(0)
    ld_ssm[0].wait()
    scan_step(0)
    rs_last(1, z_first, z_second, zb)
    gate()
    for cp in ld_wi1:
        cp.wait()
    wo[0].relay()
    wi[0].own()
    wo[0].done()
    cp = out_proj(0)
    out_sums(0, cp)
    out_reduce(0)

    for cp in (*r0_cp, *nw_cp):
        cp.wait_recv()
    r1 = r0g[...] + R["delta"][...]
    ms = jnp.sum(jnp.sum(r1 * r1, axis=2, keepdims=True), axis=0, keepdims=True) / d_model
    hg = R["hg"]
    hg[j] = (r1 * lax.rsqrt(ms + NORM_EPS) * nw1[...]).astype(BF16)

    gather_ty(hg)
    wi[0].relay()
    wi[1].own()
    wi[0].done()

    def in_proj(k, out):
        acc = None
        for i in range(nt):
            d = jnp.dot(hg[:, i].reshape(rt, dm), R["wi_g"][k, i], preferred_element_type=F32)
            acc = d if acc is None else acc + d
        out[...] = acc.astype(BF16)

    in_proj(0, xib.at[1])
    conv_proj(1)
    cp = p_pair(1)
    cps = p_cross(1, cp)
    p_finish(1, cps)
    wi[1].relay()
    wo[1].own()
    deltas(1)
    ld_ssm[1].wait()
    scan_step(1)
    wi[1].done()
    in_proj(1, zb)
    gate()
    wo[1].relay()
    wo[1].done()
    cp = out_proj(1)
    out_sums(1, cp)
    out_reduce(1)

    fin, dst = R["fin"], R["dst"]
    dst[...] = R["delta"][...].astype(BF16)
    last = [send(dst.at[p], fin.at[j, t], tx=p) for p in (tr, to, tl)]
    fin[j, t] = dst[t]
    for cp in last:
        cp.wait_recv()
    gather_ty(fin)
    outs.append(local(fin, R["fin_out"]))

    for cp in outs:
        cp.wait()
    for cp in sent:
        cp.wait_send()


def state_kernel(n_state, ssm, dt, xc, bt, a_log, conv, xi, r0, fin, ssm_out, conv_out, r_out):
    neg_a = -jnp.exp(a_log[0])
    rows = dt.shape[1]
    for g in range(rows // 8):
        sl = slice(g * 8, (g + 1) * 8)
        b_all = bt[0, g]
        dt8 = dt[0, sl, :]
        dx8 = dt8 * xc[0, sl, :].astype(F32)
        for b in range(8):
            s = ssm[0, g * 8 + b]
            b_col = jnp.broadcast_to(b_all[:n_state, b:b + 1], s.shape)
            ssm_out[0, g * 8 + b] = jnp.exp(dt8[b:b + 1, :] * neg_a) * s + dx8[b:b + 1, :] * b_col
    conv_out[0, 0] = conv[0, 1]
    conv_out[0, 1] = conv[0, 2]
    conv_out[0, 2] = xi[0]
    rj = fin.shape[2]
    for q in range(fin.shape[0]):
        sl = slice(q * rj, (q + 1) * rj)
        r_out[sl, :] = r0[sl, :] + fin[q, 0].astype(F32)


def solution(mesh):
    nt, nj = mesh.shape["tx"], mesh.shape["ty"]

    def local_step(residual, norm_w, w_in, conv_w, conv_b, w_x, w_dt, dt_bias, a_log, d_skip, w_out, conv_state, ssm_state):
        n_l, rt, ch, n_state = ssm_state.shape
        rows_all, dm = residual.shape
        n_px = w_x.shape[-1]
        half, rj = rt // 2, rt // nj
        w_in_k = jnp.transpose(w_in, (0, 2, 1, 3))
        conv_w_t = jnp.transpose(conv_w, (0, 2, 1))
        a_log_t = jnp.transpose(a_log, (0, 2, 1))
        conv_t = jnp.transpose(conv_state, (0, 3, 1, 2))
        ssm_t = jnp.transpose(ssm_state, (0, 1, 3, 2))
        w_dt_p = jnp.pad(w_dt, ((0, 0), (0, n_px - w_dt.shape[1]), (0, 0)))

        vm = pl.BlockSpec(memory_space=pltpu.VMEM)
        hb = pl.BlockSpec(memory_space=pl.ANY)
        ins = [("r0", residual, vm), ("nw", norm_w, vm), ("conv_w", conv_w_t, vm), ("conv_b", conv_b, vm),
               ("dt_bias", dt_bias, vm), ("d_skip", d_skip, vm), ("a_log", a_log_t, vm),
               ("w_in", w_in_k, hb), ("w_x", w_x, hb), ("w_dt", w_dt_p, hb), ("w_out", w_out, hb),
               ("conv_state", conv_t, hb), ("ssm", ssm_t, hb)]
        S = jax.ShapeDtypeStruct
        outs = [("fin_out", S((nj, nt, rj, dm), BF16)), ("xi_out", S((n_l, rt, ch), BF16)), ("xc_out", S((n_l, rt, ch), BF16)),
                ("dt_out", S((n_l, rt, ch), F32)), ("bt_out", S((n_l, rt // 8, 2 * n_state, half), F32))]
        V = pltpu.VMEM
        scratch = [("w0", V((2, dm, ch), BF16)), ("convs", V((n_l, 3, rt, ch), BF16)), ("wx", V((n_l, ch, n_px), BF16)),
                   ("wdt", V((n_l, n_px, ch), BF16)), ("wo_g", V((n_l, nt, ch, dm), BF16)), ("wi_g", V((2, nt, dm, ch), BF16)),
                   ("st", V((n_l, rt, n_state, ch), F32)), ("stat", V((rows_all // 128, 128), F32)),
                   ("stat_rx", V((nt - 1, rows_all // 128, 128), F32)), ("h0", V((rows_all, dm), BF16)),
                   ("pf", V((2, rows_all, ch), F32)), ("stg", V((2, rows_all, ch), BF16)), ("fac", V((rows_all, 128), F32)),
                   ("rx", V((2, 6, half, ch), BF16)), ("tx2", V((2, 2, half, ch), BF16)),
                   ("nw1_g", V((nt, 1, dm), F32)), ("r0g", V((nt, rj, dm), F32)),
                   ("xib", V((n_l, rt, ch), BF16)), ("zb", V((rt, ch), BF16)), ("xcf", V((rt, ch), F32)), ("xcb", V((n_l, rt, ch), BF16)),
                   ("px", V((rt, n_px), F32)), ("pst", V((n_l, rt, n_px), BF16)), ("pr0", V((n_l, half, n_px), BF16)),
                   ("pr1", V((n_l, 3, half, n_px), BF16)), ("pr2", V((n_l, half, n_px), BF16)), ("qs", V((n_l, half, n_px), BF16)),
                   ("tot", V((n_l, half, n_px), BF16)), ("dtb", V((n_l, rt, ch), F32)),
                   ("btg", V((n_l, rt // 8, 2 * n_state, half), F32)), ("ys", V((rt, ch), F32)), ("yb", V((rt, ch), BF16)),
                   ("of", V((nj, nt, rj, dm), F32)), ("ost", V((n_l, 2, nj // 2, nt, rj, dm), BF16)),
                   ("opr", V((n_l, nj // 2, nt, rj, dm), BF16)), ("css", V((n_l, nj // 2, nt, rj, dm), BF16)),
                   ("sums", V((nj // 2, nt, rj, dm), F32)), ("rxs", V((n_l, 6, nt // 2, rj, dm), BF16)),
                   ("tx2s", V((n_l, 2, nt // 2, rj, dm), BF16)), ("delta", V((nt, rj, dm), F32)),
                   ("hg", V((nj, nt, rj, dm), BF16)), ("fin", V((nj, nt, rj, dm), BF16)), ("dst", V((nt, rj, dm), BF16)),
                   ("send_sem", pltpu.SemaphoreType.DMA((88,))), ("recv_sem", pltpu.SemaphoreType.DMA((88,))),
                   ("loc_sem", pltpu.SemaphoreType.DMA((24,)))]
        names = [n for n, *_ in ins] + [n for n, _ in outs] + [n for n, _ in scratch]
        fin, xi, xc, dt, bt = pl.pallas_call(
            functools.partial(mixer_kernel, names, nt, nj, n_state),
            out_shape=[s for _, s in outs],
            in_specs=[s for _, _, s in ins],
            out_specs=[hb] * len(outs),
            scratch_shapes=[s for _, s in scratch],
            compiler_params=pltpu.CompilerParams(collective_id=0, has_side_effects=True, vmem_limit_bytes=60 * 2**20),
            name="mixer",
        )(*[a for _, a, _ in ins])

        rb = 32
        n_b = rt // rb
        rr = rows_all // (n_l * n_b)
        qj = rr // rj
        per_t = rt // rr
        ssm_new, conv_new, r_new = pl.pallas_call(
            functools.partial(state_kernel, n_state),
            grid=(n_l, n_b),
            in_specs=[pl.BlockSpec((1, rb, n_state, ch), lambda l, b: (l, b, 0, 0)),
                      pl.BlockSpec((1, rb, ch), lambda l, b: (l, b, 0)),
                      pl.BlockSpec((1, rb, ch), lambda l, b: (l, b, 0)),
                      pl.BlockSpec((1, rb // 8, 2 * n_state, half), lambda l, b: (l, b, 0, 0)),
                      pl.BlockSpec((1, n_state, ch), lambda l, b: (l, 0, 0)),
                      pl.BlockSpec((1, 3, rb, ch), lambda l, b: (l, 0, b, 0)),
                      pl.BlockSpec((1, rb, ch), lambda l, b: (l, b, 0)),
                      pl.BlockSpec((rr, dm), lambda l, b: (l * n_b + b, 0)),
                      pl.BlockSpec((qj, 1, rj, dm), lambda l, b: (lax.rem(l * n_b + b, per_t), (l * n_b + b) // per_t, 0, 0))],
            out_specs=[pl.BlockSpec((1, rb, n_state, ch), lambda l, b: (l, b, 0, 0)),
                       pl.BlockSpec((1, 3, rb, ch), lambda l, b: (l, 0, b, 0)),
                       pl.BlockSpec((rr, dm), lambda l, b: (l * n_b + b, 0))],
            out_shape=[S(ssm_t.shape, F32), S(conv_t.shape, BF16), S((rows_all, dm), F32)],
            compiler_params=pltpu.CompilerParams(dimension_semantics=("arbitrary", "arbitrary")),
            name="state",
        )(ssm_t, dt, xc, bt, a_log_t, conv_t, xi, residual, fin)
        return r_new, jnp.transpose(conv_new, (0, 2, 3, 1)), jnp.transpose(ssm_new, (0, 1, 3, 2))

    cache_spec = P(None, ("dp", "tx"), "ty", None)
    in_specs = (P("dp", "tx"), P(None, "tx"), P(None, "tx", None, "ty"), P(None, "ty", None), P(None, "ty"), P(None, "ty", None), P(None, None, "ty"), P(None, "ty"), P(None, "ty", None), P(None, "ty"), P(None, "ty", "tx"), cache_spec, cache_spec)
    out_specs = (P("dp", "tx"), cache_spec, cache_spec)
    return jax.shard_map(local_step, mesh=mesh, in_specs=in_specs, out_specs=out_specs, check_vma=False)
```

time: 385 us -> 137 us (0.36)
  waiting for transfers between devices: 256 us -> 0 us
  Pallas kernels: 0 us -> 132 us
  other arithmetic: 46.6 us -> 0 us
  blocking collectives: 42.3 us -> 0 us
  matrix products: 15.6 us -> 0 us
  between operations: 14.5 us -> 0.64 us
    psum x4 -> x0, waiting for transfers between devices: 211 us -> none  [sum_over_ty(): return lax.psum(part_sum.astype(jnp.bfloat16), 'ty').astype(jnp.float32)]
    pallas_call x0 -> x2, Pallas kernels: none -> 132 us  [the longest x1 114 us: local_step(): pl.pallas_call(functools.partial(mixer_kernel, names, nt, nj, n_state), o...]
    reduce_scatter x2 -> x0, waiting for transfers between devices: 44.9 us -> none  [local_step(): lax.psum_scatter(proj_part.astype(jnp.bfloat16), 'tx', scatter_dimension=...]
    all_gather x2 -> x0, blocking collectives: 22.4 us -> none  [local_step(): gated_rows = lax.all_gather(gated, 'tx', axis=0, tiled=True)]
    psum x2 -> x0, blocking collectives: 19.9 us -> none  [local_step(): sq_total = lax.psum(sq_part, 'tx')]
    add x2 -> x0, other arithmetic: 15.8 us -> none  [the longest x1 13.3 us: channel_update(): decay * ssm_prev + (delta * x_float)[:, :, None] * b_mat[:, None, :]]
    dot_general x8 -> x0, matrix products: 15.6 us -> none  [the longest x2 7.09 us: local_step(): jnp.einsum('bd,dke->bke', normed, w_in[layer_idx], preferred_element_type...]
    another operation x4 -> x0, other arithmetic: 13.4 us -> none  [local_step(): return (residual, jnp.stack(conv_list), jnp.stack(ssm_list))]
  transfers between devices with their start and end apart: 6 -> 0, of which waited for: 6 -> 0; matrix products, arithmetic and copies ran while one was open for 4% -> 0% of each run, Pallas kernels for 0% -> 0%
where the time goes in v1:
time: 137 us; the launch traced here: 136 us
  Pallas kernels  132 us (96%)
  local copies, waits for them, and re-layouts  4.04 us (3%)
    pallas_call x1, Pallas kernels, local_step(): pl.pallas_call(functools.partial(mixer_kernel, names, nt, nj, n_state), o...  114 us
    pallas_call x1, Pallas kernels, local_step(): pl.pallas_call(functools.partial(state_kernel, n_state), grid=(n_l, n_b),...  18 us

profile of v1, /device:TPU:97, one launch (start us, length us, event | category | flops | bytes accessed | tf_op | source)
XLA Modules:
  0.0 136.5 jit_solution(12278648242581555396)
XLA Ops:
  0.6 1.6 %pad.4.refs_9_ = bf16[2,128,384]{2,1,0:T(8,128)(2,1)} pad(bf16[2,96,384]{2,1,0:T(8,128)(2,1)} %param.19, bf16[]{:T(256)} %constant.2.clone.1), padding=0_0x0_32x0_0 | pad | bytes 344066 | tf_op jit(solution)/shard_map/jit(_pad)/pad | solution.py:478
  2.2 2.4 %copy.18 = bf16[2,384,2,384]{3,1,2,0:T(8,128)(2,1)} copy(bf16[2,384,2,384]{3,2,1,0:T(2,128)(2,1)} %param.15) | data formatting | bytes 2359296 | tf_op args[2]
  4.7 113.8 %mixer.1 = (bf16[8,4,32,384]{3,2,1,0:T(8,128)(2,1)}, bf16[2,256,384]{2,1,0:T(8,128)(2,1)}, bf16[2,256,384]{2,1,0:T(8,128)(2,1)}, f32[2,256,384]{2,1,0:T(8,128)}, f32[2,32,32,128]{3,2,1,0:T(8,128)}) custom-call(f32[1024,384]{1,0:T(8,128)} %r0.1, f32[2,384]{1,0:T(2,128)} %refs_1_.1, f32[2,4,384]{2,1,0:T(4,128)} %bitcast.16, f32[2,384]{1,0:T(2,128)} %refs_3_.1, ...), custom_call_target="tpu_custom_call" | custom-call | tf_op jit(solution)/shard_map/mixer/pallas_call | solution.py:510
  118.4 18.0 %state.1 = (f32[2,256,16,384]{3,2,1,0:T(8,128)}, bf16[2,3,256,384]{3,2,1,0:T(8,128)(2,1)}, f32[1024,384]{1,0:T(8,128)}) custom-call(f32[2,256,16,384]{3,2,1,0:T(8,128)} %bitcast.10, f32[2,256,384]{2,1,0:T(8,128)} %get-tuple-element.11.dt, bf16[2,256,384]{2,1,0:T(8,128)(2,1)} %get-tuple-element.12.xc, f32[2,32,32,128]{3,2,1,0:T(8,128)} %get-tuple-element.13.bt, ...), custom_call_target="tpu_custom_call" | custom-call | tf_op jit(solution)/shard_map/state/pallas_call | solution.py:525

commit v2 on v1

v2 whole, which is shorter than its diff:
```python
import functools

import jax
import jax.numpy as jnp
from jax import lax
from jax.experimental import pallas as pl
from jax.experimental.pallas import tpu as pltpu
from jax.sharding import PartitionSpec as P

NORM_EPS = 1e-5
INNER_EPS = 1e-6
LOG2E = 1.4426950408889634
MESH = pl.DeviceIdType.MESH
F32 = jnp.float32
BF16 = jnp.bfloat16


def silu(v):
    return v * jax.nn.sigmoid(v)


def softplus(v):
    return jnp.maximum(v, 0.0) + jnp.log1p(jnp.exp(-jnp.abs(v)))


def loop(n, body):
    def step(i, carry):
        body(i)
        return carry

    lax.fori_loop(0, n, step, 0)


def fold_rows(vs):
    row = lax.broadcasted_iota(jnp.int32, vs[0].shape, 0)
    k = 1
    while len(vs) > 1:
        low = (row & k) == 0
        vs = [jnp.where(low, a, b) + pltpu.roll(jnp.where(low, b, a), 8 - k, 0) for a, b in zip(vs[::2], vs[1::2])]
        k *= 2
    return vs[0]


def mixer_kernel(names, nt, nj, n_state, *refs):
    R = dict(zip(names, refs))
    r0, nw, conv_w, conv_b = R["r0v"], R["nwv"], R["conv_wv"], R["conv_bv"]
    dt_bias, d_skip, a_log = R["dt_biasv"], R["d_skipv"], R["a_logv"]
    rows_all, dm = r0.shape
    ch = a_log.shape[-1]
    rt = rows_all // nt
    half = rt // 2
    rj = rt // nj
    n_rank = R["px"].shape[-1] - 2 * n_state
    d_model = dm * nt

    t = lax.axis_index("tx")
    j = lax.axis_index("ty")
    tr, to, tl = lax.rem(t + 1, nt), lax.rem(t + 2, nt), lax.rem(t + 3, nt)
    core = lax.rem(j, 2)
    jp = j + 1 - 2 * core
    jr, jo, jl = lax.rem(j + 2, nj), lax.rem(j + 4, nj), lax.rem(j + 6, nj)
    x, xr, xo, xl = j // 2, jr // 2, jo // 2, jl // 2

    count = {"r": 0, "l": 0}
    sent = []

    def send(src, dst, **dev):
        i = count["r"]
        count["r"] += 1
        cp = pltpu.make_async_remote_copy(
            src_ref=src, dst_ref=dst, send_sem=R["send_sem"].at[i], recv_sem=R["recv_sem"].at[i],
            device_id=dev, device_id_type=MESH)
        cp.start()
        sent.append(cp)
        return cp

    def local(src, dst):
        i = count["l"]
        count["l"] += 1
        cp = pltpu.make_async_copy(src, dst, R["loc_sem"].at[i])
        cp.start()
        return cp

    barrier = pltpu.get_barrier_semaphore()
    for peer in (tr, to, tl):
        pl.semaphore_signal(barrier, inc=1, device_id={"tx": peer}, device_id_type=MESH)
    for peer in (jp, jr, jo, jl):
        pl.semaphore_signal(barrier, inc=1, device_id={"ty": peer}, device_id_type=MESH)

    ld_r0 = [local(R["r0"], r0), local(R["nw"], nw)]
    ld_win0 = local(R["w_in"].at[0], R["w0"])
    ld_small = [local(R[n], R[n + "v"]) for n in ("conv_w", "conv_b", "dt_bias", "d_skip", "a_log")]
    ld_conv = [local(R["conv_state"].at[l, 0], R["convs"].at[l]) for l in range(2)]
    ld_conv += [local(R["conv_state"].at[l, pl.ds(1, 2)], R["conv_out"].at[l, pl.ds(0, 2)]) for l in range(2)]
    ld_wx = local(R["w_x"], R["wx"])
    R["wdt"][:, n_rank:, :] = jnp.zeros_like(R["wdt"][:, n_rank:, :])
    ld_wdt = local(R["w_dt"], R["wdt"].at[:, pl.ds(0, n_rank)])
    ld_wo = [local(R["w_out"].at[l], R["wo_g"].at[l, t]) for l in range(2)]
    ld_wi1 = [local(R["w_in"].at[1, k], R["wi_g"].at[k, t]) for k in range(2)]
    ld_ssm = [local(R["ssm"].at[l], R["ssm_out"].at[l]) for l in range(2)]

    for cp in ld_r0:
        cp.wait()

    def stat_body(b):
        rows = pl.ds(pl.multiple_of(b * 128, 128), 128)
        r = r0[rows, :]
        sq = r * r
        part = sq[:, :128]
        for i in range(1, dm // 128):
            part = part + sq[:, i * 128:(i + 1) * 128]
        R["stat"][pl.ds(b, 1), :] = jnp.sum(part.T, axis=0, keepdims=True)
        col = jnp.sum(part, axis=1, keepdims=True)
        lr = lax.rsqrt(col / dm + NORM_EPS)
        R["h0"][rows, :] = (r * lr * nw[0:1, :]).astype(BF16)

    loop(rows_all // 128, stat_body)
    ld_win0.wait()
    pf, stg = R["pf"], R["stg"]

    def mm(k):
        def body(b):
            rows = pl.ds(pl.multiple_of(b * rt, rt), rt)
            v = jnp.dot(R["h0"][rows, :], R["w0"][k], preferred_element_type=F32)
            pf[k, rows, :] = v
            stg[k, rows, :] = v.astype(BF16)

        loop(nt, body)

    mm(0)
    rx, tx2 = R["rx"], R["tx2"]
    pl.semaphore_wait(barrier, 7)
    stats = [send(R["stat"], R["stat_rx"].at[i], tx=p) for i, p in enumerate((tr, to, tl))]

    def part_rows(owner, h):
        return pl.ds(pl.multiple_of(owner * rt + h * half, half), half)

    def rs_first(k):
        return (send(stg.at[k, part_rows(to, 0)], rx.at[k, 0], tx=tr),
                send(stg.at[k, part_rows(to, 1)], rx.at[k, 1], tx=tl),
                send(stg.at[k, part_rows(tl, 0)], rx.at[k, 2], tx=tl),
                send(stg.at[k, part_rows(tr, 1)], rx.at[k, 3], tx=tr))

    def factors():
        picks = ((0, 2 * tr), (None, 2 * tr), (2, 2 * tl + 1), (None, 2 * tl + 1), (None, 2 * t), (2, 2 * t), (None, 2 * t + 1), (0, 2 * t + 1))
        for i, (slot, blk) in enumerate(picks):
            own = R["stat"][pl.ds(blk, 1), :]
            tot = own
            for q in range(nt - 1):
                tot = tot + R["stat_rx"][q, pl.ds(blk, 1), :]
            src = own if slot is None else R["stat_rx"][slot, pl.ds(blk, 1), :]
            f = lax.rsqrt(tot / d_model + NORM_EPS) * jnp.sqrt(src / dm + NORM_EPS)
            R["fac"][i] = jnp.broadcast_to(f, (half, half)).T

    def scaled(v, i):
        return v.astype(F32) * jnp.concatenate([R["fac"][i]] * (ch // half), axis=1)

    def rs_second(k, first):
        first[0].wait_recv()
        tx2[k, 0] = (scaled(rx[k, 0], 0) + scaled(pf[k, part_rows(tr, 0), :], 1)).astype(BF16)
        a = send(tx2.at[k, 0], rx.at[k, 4], tx=tr)
        first[1].wait_recv()
        tx2[k, 1] = (scaled(rx[k, 1], 2) + scaled(pf[k, part_rows(tl, 1), :], 3)).astype(BF16)
        b = send(tx2.at[k, 1], rx.at[k, 5], tx=tl)
        return a, b

    def rs_last(k, first, second, out):
        for cp in (first[2], first[3], *second):
            cp.wait_recv()
        for h in range(2):
            v = scaled(pf[k, part_rows(t, h), :], 4 + 2 * h) + scaled(rx[k, 2 + h], 5 + 2 * h) + rx[k, 4 + h].astype(F32)
            out[h * half:(h + 1) * half, :] = v.astype(BF16)

    x_first = rs_first(0)
    mm(1)
    for cp in stats:
        cp.wait_recv()
    factors()
    x_second = rs_second(0, x_first)
    z_first = rs_first(1)

    class Gather:
        def __init__(self, buf):
            self.buf, self.half = buf, buf.shape[1] // 2

        def half_send(self, owner, hi, peer):
            part = self.buf.at[owner, pl.ds(hi * self.half, self.half)]
            return send(part, part, tx=peer)

        def own(self):
            self.a = [self.half_send(t, h, tr) for h in (0, 1)]
            self.b = [self.half_send(t, h, tl) for h in (1, 0)]

        def relay(self):
            self.a[0].wait_recv()
            self.c = self.half_send(tl, 0, tr)
            self.b[0].wait_recv()
            self.d = self.half_send(tr, 1, tl)

        def done(self):
            for cp in (self.a[1], self.b[1], self.c, self.d):
                cp.wait_recv()

    wo = [Gather(R["wo_g"].at[l]) for l in range(2)]
    wi = [Gather(R["wi_g"].at[k]) for k in range(2)]
    zb, xcf, xcb = R["zb"], R["xcf"], R["xcb"]
    caches = R["conv_out"]

    def conv_proj(l):
        def body(b):
            rows = pl.ds(pl.multiple_of(b * 32, 32), 32)
            v = R["convs"][l, rows, :].astype(F32) * conv_w[l, 0:1, :]
            for i in range(3):
                v = v + caches[l, i, rows, :].astype(F32) * conv_w[l, i + 1:i + 2, :]
            xc = silu(v + conv_b[l:l + 1, :]).astype(BF16)
            xcb[rows, :] = xc
            xcf[rows, :] = xc.astype(F32)

        loop(rt // 32, body)
        p = jnp.dot(xcb[...], R["wx"][l], preferred_element_type=F32)
        R["px"][...] = p
        R["pst"][l] = p.astype(BF16)

    def half_rows(c):
        return pl.ds(pl.multiple_of(c * half, half), half)

    def p_pair(l):
        return send(R["pst"].at[l, half_rows(1 - core)], R["pr0"].at[l], ty=jp)

    def p_cross(l, cp):
        cp.wait_recv()
        q = R["px"][half_rows(core), :] + R["pr0"][l].astype(F32)
        R["px"][half_rows(core), :] = q
        R["qs"][l] = q.astype(BF16)
        return [send(R["qs"].at[l], R["pr1"].at[l, i], ty=p) for i, p in enumerate((jr, jo, jl))]

    def p_scan(l, cps, between=None):
        for cp in cps:
            cp.wait_recv()
        q = R["px"][half_rows(core), :]
        for i in range(3):
            q = q + R["pr1"][l, i].astype(F32)
        R["px"][half_rows(core), :] = q
        R["tot"][l] = q.astype(BF16)
        cp = send(R["tot"].at[l], R["pr2"].at[l], ty=jp)
        deltas(l, core)
        scan_step(l, core)
        if between is not None:
            between()
        cp.wait_recv()
        R["px"][half_rows(1 - core), :] = R["pr2"][l].astype(F32)
        deltas(l, 1 - core)
        scan_step(l, 1 - core)

    def deltas(l, h):
        if True:
            rows = half_rows(h)
            p = R["px"][rows, :]
            lane = lax.broadcasted_iota(jnp.int32, p.shape, 1)
            is_dt = lane < n_rank
            is_b = jnp.logical_and(lane >= n_rank, lane < n_rank + n_state)
            sq = p * p

            def scale_of(mask, n):
                tot = jnp.sum(jnp.where(mask, sq, 0.0), axis=1, keepdims=True)
                return lax.rsqrt(tot / n + INNER_EPS)

            s_dt = scale_of(is_dt, n_rank)
            s_b = scale_of(is_b, n_state)
            s_c = scale_of(lane >= n_rank + n_state, n_state)
            pn = p * jnp.where(is_dt, s_dt, jnp.where(is_b, s_b, s_c))
            low = jnp.where(is_dt, pn, 0.0).astype(BF16)
            raw = jnp.dot(low, R["wdt"][l], preferred_element_type=F32) + dt_bias[l:l + 1, :]
            R["dtb"][rows, :] = softplus(raw)
            bc = pn.T[n_rank:, :]
            for g in range(half // 8):
                R["btg"][h * (half // 8) + g] = pltpu.roll(bc, (half - 8 * g) % half, 1)

    def scan_step(l, h):
        neg_a = -jnp.exp(a_log[l]) * LOG2E
        skip = d_skip[l:l + 1, :]

        def body(i):
            g = h * (half // 8) + i
            rows = pl.ds(pl.multiple_of(g * 8, 8), 8)
            bt = R["btg"][g]
            dt8 = R["dtb"][rows, :]
            xc8 = xcf[rows, :]
            dx8 = dt8 * xc8
            ys = []
            for b in range(8):
                s = R["ssm_out"][l, g * 8 + b]
                b_col = jnp.broadcast_to(bt[:n_state, b:b + 1], s.shape)
                c_col = jnp.broadcast_to(bt[n_state:, b:b + 1], s.shape)
                s = jnp.exp2(dt8[b:b + 1, :] * neg_a) * s + dx8[b:b + 1, :] * b_col
                R["ssm_out"][l, g * 8 + b] = s
                v = s * c_col
                ys.append(v[:8] + v[8:])
            R["ys"][rows, :] = fold_rows(ys) + skip * xc8

        loop(half // 8, body)

    def gate():
        def body(b):
            rows = pl.ds(pl.multiple_of(b * 32, 32), 32)
            R["yb"][rows, :] = (R["ys"][rows, :] * silu(zb[rows, :].astype(F32))).astype(BF16)

        loop(rt // 32, body)

    of, ost, css, sums = R["of"], R["ost"], R["css"], R["sums"]

    lo, hi = pl.ds(0, nt // 2), pl.ds(nt // 2, nt // 2)

    def out_reduce(l, between=None):
        pair = []
        for i in range(nt):
            o = jnp.dot(R["yb"][...], R["wo_g"][l, i], preferred_element_type=F32)
            for q in range(nj):
                v = o[q * rj:(q + 1) * rj, :]
                of[q, i] = v
                ost[l, q % 2, i, q // 2] = v.astype(BF16)
            pair.append(send(ost.at[l, 1 - core, i], R["opr"].at[l, i], ty=jp))
        ra, rb = R["rxs"], R["tx2s"]

        def chip_sum(i):
            pair[i].wait_recv()

            def body(q):
                v = of[2 * q + core, i] + R["opr"][l, i, q].astype(F32)
                sums[q, i] = v
                css[l, q, i] = v.astype(BF16)

            loop(nj // 2, body)

        chip_sum(0)
        chip_sum(1)
        c0 = send(css.at[l, xo, lo], ra.at[l, 0], ty=jr)
        c2 = send(css.at[l, xl, lo], ra.at[l, 2], ty=jl)
        chip_sum(2)
        chip_sum(3)
        c1 = send(css.at[l, xo, hi], ra.at[l, 1], ty=jl)
        c3 = send(css.at[l, xr, hi], ra.at[l, 3], ty=jr)
        c0.wait_recv()
        rb[l, 0] = (ra[l, 0].astype(F32) + sums[xr, lo]).astype(BF16)
        c4 = send(rb.at[l, 0], ra.at[l, 4], ty=jr)
        c1.wait_recv()
        rb[l, 1] = (ra[l, 1].astype(F32) + sums[xl, hi]).astype(BF16)
        c5 = send(rb.at[l, 1], ra.at[l, 5], ty=jl)
        if between is not None:
            between()
        for cp in (c2, c3, c4, c5):
            cp.wait_recv()
        d = R["delta"]
        for h, part in enumerate((lo, hi)):
            v = sums[x, part] + ra[l, 2 + h].astype(F32) + ra[l, 4 + h].astype(F32)
            if l:
                v = v + d[part]
            d[part] = v

    def gather_ty(buf, between=None):
        def part(owner, p, peer):
            return send(buf.at[owner, p], buf.at[owner, p], ty=peer)

        a = [part(j, p, jr) for p in (lo, hi)]
        b = [part(j, p, jl) for p in (hi, lo)]
        waits = [send(buf.at[j], buf.at[j], ty=jp)]
        a[0].wait_recv()
        c = part(jl, lo, jr)
        waits.append(part(jl, lo, jp))
        b[0].wait_recv()
        d = part(jr, hi, jl)
        waits.append(part(jr, hi, jp))
        a[1].wait_recv()
        waits.append(part(jl, hi, jp))
        b[1].wait_recv()
        waits.append(part(jr, lo, jp))
        if between is not None:
            between()
        c.wait_recv()
        waits.append(part(jo, lo, jp))
        d.wait_recv()
        waits.append(part(jo, hi, jp))
        for cp in waits:
            cp.wait_recv()

    for cp in (*ld_conv, ld_wx, *ld_small):
        cp.wait()
    rs_last(0, x_first, x_second, caches.at[0, 2])
    conv_proj(0)
    cp = p_pair(0)
    cps = p_cross(0, cp)
    z_second = rs_second(1, z_first)
    for cp in ld_wo:
        cp.wait()
    wo[0].own()
    nw1 = R["nw1_g"]
    nw1[t] = nw[1:2, :]
    nw_cp = [send(nw1.at[t], nw1.at[t], tx=p) for p in (tr, to, tl)]
    r0g = R["r0g"]
    r0_cp = []
    for p in (tr, to, tl):
        src = r0.at[pl.ds(pl.multiple_of(p * rt + j * rj, rj), rj)]
        r0_cp.append(send(src, r0g.at[t], tx=p))
    r0g[t] = r0[pl.ds(pl.multiple_of(t * rt + j * rj, rj), rj), :]
    ld_wdt.wait()
    ld_ssm[0].wait()
    p_scan(0, cps)
    rs_last(1, z_first, z_second, zb)
    gate()
    for cp in ld_wi1:
        cp.wait()
    wo[0].relay()
    wi[0].own()
    wo[0].done()
    def next_gate_weights():
        wi[0].relay()
        wi[1].own()

    out_reduce(0, next_gate_weights)

    for cp in (*r0_cp, *nw_cp):
        cp.wait_recv()
    r1 = r0g[...] + R["delta"][...]
    ms = jnp.sum(jnp.sum(r1 * r1, axis=2, keepdims=True), axis=0, keepdims=True) / d_model
    hg = R["hg"]
    hg[j] = (r1 * lax.rsqrt(ms + NORM_EPS) * nw1[...]).astype(BF16)

    def next_weights():
        wi[1].relay()
        wo[1].own()

    gather_ty(hg, next_weights)
    wi[0].done()

    def in_proj(k, out):
        acc = None
        for i in range(nt):
            d = jnp.dot(hg[:, i].reshape(rt, dm), R["wi_g"][k, i], preferred_element_type=F32)
            acc = d if acc is None else acc + d
        out[...] = acc.astype(BF16)

    in_proj(0, caches.at[1, 2])
    conv_proj(1)
    cp = p_pair(1)
    cps = p_cross(1, cp)
    ld_ssm[1].wait()
    p_scan(1, cps, wo[1].relay)
    wi[1].done()
    in_proj(1, zb)
    gate()
    wo[1].done()
    out_reduce(1)

    fin, dst = R["fin"], R["dst"]
    dst[...] = R["delta"][...].astype(BF16)
    last = [send(dst.at[p], fin.at[j, t], tx=p) for p in (tr, to, tl)]
    fin[j, t] = dst[t]
    for cp in last:
        cp.wait_recv()
    gather_ty(fin)

    def res_body(q):
        for i in range(nt):
            rows = pl.ds(pl.multiple_of(i * rt + q * rj, rj), rj)
            R["r_out"][rows, :] = r0[rows, :] + fin[q, i].astype(F32)

    loop(nj, res_body)
    for cp in sent:
        cp.wait_send()


def solution(mesh):
    nt, nj = mesh.shape["tx"], mesh.shape["ty"]

    def local_step(residual, norm_w, w_in, conv_w, conv_b, w_x, w_dt, dt_bias, a_log, d_skip, w_out, conv_state, ssm_state):
        n_l, rt, ch, n_state = ssm_state.shape
        rows_all, dm = residual.shape
        n_px = w_x.shape[-1]
        half, rj = rt // 2, rt // nj
        w_in_k = jnp.transpose(w_in, (0, 2, 1, 3))
        conv_w_t = jnp.transpose(conv_w, (0, 2, 1))
        a_log_t = jnp.transpose(a_log, (0, 2, 1))
        conv_t = jnp.transpose(conv_state, (0, 3, 1, 2))
        ssm_t = jnp.transpose(ssm_state, (0, 1, 3, 2))

        hb = pl.BlockSpec(memory_space=pl.ANY)
        ins = [("r0", residual, hb), ("nw", norm_w, hb), ("conv_w", conv_w_t, hb), ("conv_b", conv_b, hb),
               ("dt_bias", dt_bias, hb), ("d_skip", d_skip, hb), ("a_log", a_log_t, hb),
               ("w_in", w_in_k, hb), ("w_x", w_x, hb), ("w_dt", w_dt, hb), ("w_out", w_out, hb),
               ("conv_state", conv_t, hb), ("ssm", ssm_t, hb)]
        V = pltpu.VMEM
        outs = [("r_out", V(residual.shape, F32)), ("conv_out", V(conv_t.shape, BF16)), ("ssm_out", V(ssm_t.shape, F32))]
        scratch = [("r0v", V(residual.shape, F32)), ("nwv", V(norm_w.shape, F32)), ("conv_wv", V(conv_w_t.shape, F32)),
                   ("conv_bv", V(conv_b.shape, F32)), ("dt_biasv", V(dt_bias.shape, F32)), ("d_skipv", V(d_skip.shape, F32)),
                   ("a_logv", V(a_log_t.shape, F32)), ("w0", V((2, dm, ch), BF16)), ("convs", V((n_l, rt, ch), BF16)), ("wx", V((n_l, ch, n_px), BF16)),
                   ("wdt", V((n_l, n_px, ch), BF16)), ("wo_g", V((n_l, nt, ch, dm), BF16)), ("wi_g", V((2, nt, dm, ch), BF16)),
                   ("stat", V((rows_all // 128, 128), F32)),
                   ("stat_rx", V((nt - 1, rows_all // 128, 128), F32)), ("h0", V((rows_all, dm), BF16)),
                   ("pf", V((2, rows_all, ch), F32)), ("stg", V((2, rows_all, ch), BF16)), ("fac", V((8, half, half), F32)),
                   ("rx", V((2, 6, half, ch), BF16)), ("tx2", V((2, 2, half, ch), BF16)),
                   ("nw1_g", V((nt, 1, dm), F32)), ("r0g", V((nt, rj, dm), F32)),
                   ("zb", V((rt, ch), BF16)), ("xcf", V((rt, ch), F32)), ("xcb", V((rt, ch), BF16)),
                   ("px", V((rt, n_px), F32)), ("pst", V((n_l, rt, n_px), BF16)), ("pr0", V((n_l, half, n_px), BF16)),
                   ("pr1", V((n_l, 3, half, n_px), BF16)), ("pr2", V((n_l, half, n_px), BF16)), ("qs", V((n_l, half, n_px), BF16)),
                   ("tot", V((n_l, half, n_px), BF16)), ("dtb", V((rt, ch), F32)),
                   ("btg", V((rt // 8, 2 * n_state, half), F32)), ("ys", V((rt, ch), F32)), ("yb", V((rt, ch), BF16)),
                   ("of", V((nj, nt, rj, dm), F32)), ("ost", V((n_l, 2, nt, nj // 2, rj, dm), BF16)),
                   ("opr", V((n_l, nt, nj // 2, rj, dm), BF16)), ("css", V((n_l, nj // 2, nt, rj, dm), BF16)),
                   ("sums", V((nj // 2, nt, rj, dm), F32)), ("rxs", V((n_l, 6, nt // 2, rj, dm), BF16)),
                   ("tx2s", V((n_l, 2, nt // 2, rj, dm), BF16)), ("delta", V((nt, rj, dm), F32)),
                   ("hg", V((nj, nt, rj, dm), BF16)), ("fin", V((nj, nt, rj, dm), BF16)), ("dst", V((nt, rj, dm), BF16)),
                   ("send_sem", pltpu.SemaphoreType.DMA((120,))), ("recv_sem", pltpu.SemaphoreType.DMA((120,))),
                   ("loc_sem", pltpu.SemaphoreType.DMA((32,)))]
        names = [n for n, *_ in ins] + [n for n, _ in outs] + [n for n, _ in scratch]
        r_new, conv_new, ssm_new = pl.pallas_call(
            functools.partial(mixer_kernel, names, nt, nj, n_state),
            out_shape=[s for _, s in outs],
            in_specs=[s for _, _, s in ins],
            out_specs=[pl.BlockSpec(memory_space=V)] * len(outs),
            scratch_shapes=[s for _, s in scratch],
            compiler_params=pltpu.CompilerParams(collective_id=0, has_side_effects=True, vmem_limit_bytes=40 * 2**20),
            name="mixer",
        )(*[a for _, a, _ in ins])

        return r_new, jnp.transpose(conv_new, (0, 2, 3, 1)), jnp.transpose(ssm_new, (0, 1, 3, 2))

    cache_spec = P(None, ("dp", "tx"), "ty", None)
    in_specs = (P("dp", "tx"), P(None, "tx"), P(None, "tx", None, "ty"), P(None, "ty", None), P(None, "ty"), P(None, "ty", None), P(None, None, "ty"), P(None, "ty"), P(None, "ty", None), P(None, "ty"), P(None, "ty", "tx"), cache_spec, cache_spec)
    out_specs = (P("dp", "tx"), cache_spec, cache_spec)
    return jax.shard_map(local_step, mesh=mesh, in_specs=in_specs, out_specs=out_specs, check_vma=False)
```

time: 137 us -> 103 us (0.75)
  Pallas kernels: 132 us -> 93.1 us
  local copies, waits for them, and re-layouts: 4.04 us -> 9.37 us
    pallas_call x1, Pallas kernels: 114 us -> 93.1 us  [local_step(): pl.pallas_call(functools.partial(mixer_kernel, names, nt, nj, n_state), o...]
    pallas_call x1 -> x0, Pallas kernels: 18 us -> none  [local_step(): pl.pallas_call(functools.partial(state_kernel, n_state), grid=(n_l, n_b),...]
    unnamed x1 -> x4, local copies, waits for them, and re-layouts: 2.43 us -> 9.37 us
    pad x1 -> x0, local copies, waits for them, and re-layouts: 1.61 us -> none  [local_step(): w_dt_p = jnp.pad(w_dt, ((0, 0), (0, n_px - w_dt.shape[1]), (0, 0)))]
where the time goes in v2:
time: 103 us
  Pallas kernels  93.1 us (90%)
  local copies, waits for them, and re-layouts  9.37 us (9%)
    pallas_call x1, Pallas kernels, local_step(): pl.pallas_call(functools.partial(mixer_kernel, names, nt, nj, n_state), o...  93.1 us
    unnamed x4, local copies, waits for them, and re-layouts  9.37 us

profile of v2, /device:TPU:97, one launch (start us, length us, event | category | flops | bytes accessed | tf_op | source)
XLA Modules:
  0.0 103.1 jit_solution(3036780979273210693)
XLA Ops:
  0.6 2.4 %copy.18 = bf16[2,384,2,384]{3,1,2,0:T(8,128)(2,1)} copy(bf16[2,384,2,384]{3,2,1,0:T(2,128)(2,1)} %param.15) | data formatting | bytes 2359296 | tf_op args[2]
  3.1 93.1 %mixer.1 = (f32[1024,384]{1,0:T(8,128)S(1)}, bf16[2,3,256,384]{3,2,1,0:T(8,128)(2,1)S(1)}, f32[2,256,16,384]{3,2,1,0:T(8,128)S(1)}) custom-call(f32[1024,384]{1,0:T(8,128)} %refs_0_.1, f32[2,384]{1,0:T(2,128)} %refs_1_.1, f32[2,4,384]{2,1,0:T(4,128)} %bitcast.15, f32[2,384]{1,0:T(2,128)} %refs_3_.1, f32[2,384]{1,0:T(2,128)} %refs_4_.1, f32[2,384]{1,0:T(2,128)} %refs_5_.1, ...), custom_call_target="tpu_custom_call" | custom-call | tf_op jit(solution)/shard_map/mixer/pallas_call | solution.py:515
  96.2 1.1 %copy.22 = f32[1024,384]{1,0:T(8,128)} copy(f32[1024,384]{1,0:T(8,128)S(1)} %get-tuple-element.9) | data formatting | bytes 3145728
  97.3 1.0 copy.23
  98.3 4.8 %copy.24 = f32[2,256,384,16]{2,3,1,0:T(8,128)} copy(f32[2,256,384,16]{2,3,1,0:T(8,128)S(1)} %bitcast.9) | data formatting | bytes 25165824

commit v3 on v2

--- a/solution.py
+++ b/solution.py
@@ -1,4 +1,5 @@
 import functools
+import math
 
 import jax
 import jax.numpy as jnp
@@ -61,17 +62,28 @@
     jr, jo, jl = lax.rem(j + 2, nj), lax.rem(j + 4, nj), lax.rem(j + 6, nj)
     x, xr, xo, xl = j // 2, jr // 2, jo // 2, jl // 2
 
-    count = {"r": 0, "l": 0}
-    sent = []
+    count = {"r": 0, "l": 0, "s": 0, 0: 0, 1: 0, 2: 0}
+    single = []
+    drain = (R["ssm_out"].at[0], R["ssm_out"].at[0], R["btg"])
+    unit = (n_state * ch * 4, n_state * ch * 4, 2 * n_state * half * 4)
 
     def send(src, dst, **dev):
         i = count["r"]
         count["r"] += 1
+        size = math.prod(src.shape) * jnp.dtype(src.dtype).itemsize
+        kind = next((k for k in range(3) if size % unit[k] == 0 and count[k] + size // unit[k] <= drain[k].shape[0]), None)
+        if kind is None:
+            sem = R["small_sem"].at[count["s"]]
+            count["s"] += 1
+        else:
+            sem = R["send_sem"].at[kind]
+            count[kind] += size // unit[kind]
         cp = pltpu.make_async_remote_copy(
-            src_ref=src, dst_ref=dst, send_sem=R["send_sem"].at[i], recv_sem=R["recv_sem"].at[i],
+            src_ref=src, dst_ref=dst, send_sem=sem, recv_sem=R["recv_sem"].at[i],
             device_id=dev, device_id_type=MESH)
         cp.start()
-        sent.append(cp)
+        if kind is None:
+            single.append(cp)
         return cp
 
     def local(src, dst):
@@ -87,20 +99,11 @@
     for peer in (jp, jr, jo, jl):
         pl.semaphore_signal(barrier, inc=1, device_id={"ty": peer}, device_id_type=MESH)
 
-    ld_r0 = [local(R["r0"], r0), local(R["nw"], nw)]
-    ld_win0 = local(R["w_in"].at[0], R["w0"])
-    ld_small = [local(R[n], R[n + "v"]) for n in ("conv_w", "conv_b", "dt_bias", "d_skip", "a_log")]
-    ld_conv = [local(R["conv_state"].at[l, 0], R["convs"].at[l]) for l in range(2)]
-    ld_conv += [local(R["conv_state"].at[l, pl.ds(1, 2)], R["conv_out"].at[l, pl.ds(0, 2)]) for l in range(2)]
-    ld_wx = local(R["w_x"], R["wx"])
-    R["wdt"][:, n_rank:, :] = jnp.zeros_like(R["wdt"][:, n_rank:, :])
-    ld_wdt = local(R["w_dt"], R["wdt"].at[:, pl.ds(0, n_rank)])
-    ld_wo = [local(R["w_out"].at[l], R["wo_g"].at[l, t]) for l in range(2)]
-    ld_wi1 = [local(R["w_in"].at[1, k], R["wi_g"].at[k, t]) for k in range(2)]
-    ld_ssm = [local(R["ssm"].at[l], R["ssm_out"].at[l]) for l in range(2)]
-
-    for cp in ld_r0:
-        cp.wait()
+    ld_nw = local(R["nw"], nw)
+    ld_r0 = [local(R["r0"].at[pl.ds(i * rt, rt)], r0.at[pl.ds(i * rt, rt)]) for i in range(nt)]
+    ld_win = [local(R["w_in"].at[0], R["win"].at[0])]
+
+    ld_nw.wait()
 
     def stat_body(b):
         rows = pl.ds(pl.multiple_of(b * 128, 128), 128)
@@ -114,8 +117,27 @@
         lr = lax.rsqrt(col / dm + NORM_EPS)
         R["h0"][rows, :] = (r * lr * nw[0:1, :]).astype(BF16)
 
-    loop(rows_all // 128, stat_body)
-    ld_win0.wait()
+    def split_weights(l, k, out):
+        def body(i):
+            rows = pl.ds(pl.multiple_of(i * 32, 32), 32)
+            out[rows, :] = R["win"][l, rows, k, :]
+
+        loop(dm // 32, body)
+
+    per = rt // 128
+    for i in range(nt):
+        ld_r0[i].wait()
+        loop(per, lambda b, i=i: stat_body(i * per + b))
+    ld_win.append(local(R["w_in"].at[1], R["win"].at[1]))
+    ld_conv = [local(R["conv_state"].at[l, 0], R["convs"].at[l]) for l in range(2)]
+    ld_conv += [local(R["conv_state"].at[l, pl.ds(1, 2)], R["conv_out"].at[l, pl.ds(0, 2)]) for l in range(2)]
+    ld_small = [local(R[n], R[n + "v"]) for n in ("conv_w", "conv_b", "dt_bias", "d_skip", "a_log")]
+    ld_wx = local(R["w_x"], R["wx"])
+    ld_wdt = local(R["w_dt"], R["wdt"].at[:, pl.ds(0, n_rank)])
+    ld_wo = [local(R["w_out"].at[l], R["wo_g"].at[l, t]) for l in range(2)]
+    ld_ssm = [local(R["ssm"].at[l], R["ssm_out"].at[l]) for l in range(2)]
+    ld_win[0].wait()
+    split_weights(0, 0, R["w0"].at[0])
     pf, stg = R["pf"], R["stg"]
 
     def mm(k):
@@ -172,12 +194,14 @@
             out[h * half:(h + 1) * half, :] = v.astype(BF16)
 
     x_first = rs_first(0)
+    split_weights(0, 1, R["w0"].at[1])
     mm(1)
     for cp in stats:
         cp.wait_recv()
     factors()
     x_second = rs_second(0, x_first)
     z_first = rs_first(1)
+    R["wdt"][:, n_rank:, :] = jnp.zeros_like(R["wdt"][:, n_rank:, :])
 
     class Gather:
         def __init__(self, buf):
@@ -235,19 +259,24 @@
         return [send(R["qs"].at[l], R["pr1"].at[l, i], ty=p) for i, p in enumerate((jr, jo, jl))]
 
     def p_scan(l, cps, between=None):
-        for cp in cps:
-            cp.wait_recv()
+        with jax.named_scope("P_cross_wait"):
+            for cp in cps:
+                cp.wait_recv()
         q = R["px"][half_rows(core), :]
         for i in range(3):
             q = q + R["pr1"][l, i].astype(F32)
         R["px"][half_rows(core), :] = q
         R["tot"][l] = q.astype(BF16)
         cp = send(R["tot"].at[l], R["pr2"].at[l], ty=jp)
-        deltas(l, core)
-        scan_step(l, core)
-        if between is not None:
-            between()
-        cp.wait_recv()
+        with jax.named_scope("P_deltas"):
+            deltas(l, core)
+        with jax.named_scope("P_scan"):
+            scan_step(l, core)
+        with jax.named_scope("P_between"):
+            if between is not None:
+                between()
+        with jax.named_scope("P_pair_wait"):
+            cp.wait_recv()
         R["px"][half_rows(1 - core), :] = R["pr2"][l].astype(F32)
         deltas(l, 1 - core)
         scan_step(l, 1 - core)
@@ -393,6 +422,11 @@
     for cp in ld_wo:
         cp.wait()
     wo[0].own()
+    ld_wdt.wait()
+    ld_ssm[0].wait()
+    p_scan(0, cps, wo[0].relay)
+    rs_last(1, z_first, z_second, zb)
+    gate()
     nw1 = R["nw1_g"]
     nw1[t] = nw[1:2, :]
     nw_cp = [send(nw1.at[t], nw1.at[t], tx=p) for p in (tr, to, tl)]
@@ -402,14 +436,9 @@
         src = r0.at[pl.ds(pl.multiple_of(p * rt + j * rj, rj), rj)]
         r0_cp.append(send(src, r0g.at[t], tx=p))
     r0g[t] = r0[pl.ds(pl.multiple_of(t * rt + j * rj, rj), rj), :]
-    ld_wdt.wait()
-    ld_ssm[0].wait()
-    p_scan(0, cps)
-    rs_last(1, z_first, z_second, zb)
-    gate()
-    for cp in ld_wi1:
-        cp.wait()
-    wo[0].relay()
+    ld_win[1].wait()
+    for k in range(2):
+        split_weights(1, k, R["wi_g"].at[k, t])
     wi[0].own()
     wo[0].done()
     def next_gate_weights():
@@ -465,8 +494,22 @@
             R["r_out"][rows, :] = r0[rows, :] + fin[q, i].astype(F32)
 
     loop(nj, res_body)
-    for cp in sent:
+    for cp in single:
         cp.wait_send()
+    for k in range(3):
+        taken = drain[k].at[pl.ds(0, count[k])]
+        pltpu.make_async_copy(taken, taken, R["send_sem"].at[k]).wait()
+    assert [count[c] for c in "rls"] == [R[n].shape[0] for n in ("recv_sem", "loc_sem", "small_sem")], count
+
+
+def flush_kernel(*refs):
+    n = (len(refs) - 1) // 2
+    srcs, dsts, sem = refs[:n], refs[n:2 * n], refs[2 * n]
+    cps = [pltpu.make_async_copy(s, d, sem.at[i]) for i, (s, d) in enumerate(zip(srcs, dsts))]
+    for cp in cps:
+        cp.start()
+    for cp in cps:
+        cp.wait()
 
 
 def solution(mesh):
@@ -477,7 +520,6 @@
         rows_all, dm = residual.shape
         n_px = w_x.shape[-1]
         half, rj = rt // 2, rt // nj
-        w_in_k = jnp.transpose(w_in, (0, 2, 1, 3))
         conv_w_t = jnp.transpose(conv_w, (0, 2, 1))
         a_log_t = jnp.transpose(a_log, (0, 2, 1))
         conv_t = jnp.transpose(conv_state, (0, 3, 1, 2))
@@ -486,13 +528,13 @@
         hb = pl.BlockSpec(memory_space=pl.ANY)
         ins = [("r0", residual, hb), ("nw", norm_w, hb), ("conv_w", conv_w_t, hb), ("conv_b", conv_b, hb),
                ("dt_bias", dt_bias, hb), ("d_skip", d_skip, hb), ("a_log", a_log_t, hb),
-               ("w_in", w_in_k, hb), ("w_x", w_x, hb), ("w_dt", w_dt, hb), ("w_out", w_out, hb),
+               ("w_in", w_in, hb), ("w_x", w_x, hb), ("w_dt", w_dt, hb), ("w_out", w_out, hb),
                ("conv_state", conv_t, hb), ("ssm", ssm_t, hb)]
         V = pltpu.VMEM
         outs = [("r_out", V(residual.shape, F32)), ("conv_out", V(conv_t.shape, BF16)), ("ssm_out", V(ssm_t.shape, F32))]
         scratch = [("r0v", V(residual.shape, F32)), ("nwv", V(norm_w.shape, F32)), ("conv_wv", V(conv_w_t.shape, F32)),
                    ("conv_bv", V(conv_b.shape, F32)), ("dt_biasv", V(dt_bias.shape, F32)), ("d_skipv", V(d_skip.shape, F32)),
-                   ("a_logv", V(a_log_t.shape, F32)), ("w0", V((2, dm, ch), BF16)), ("convs", V((n_l, rt, ch), BF16)), ("wx", V((n_l, ch, n_px), BF16)),
+                   ("a_logv", V(a_log_t.shape, F32)), ("win", V(w_in.shape, BF16)), ("w0", V((2, dm, ch), BF16)), ("convs", V((n_l, rt, ch), BF16)), ("wx", V((n_l, ch, n_px), BF16)),
                    ("wdt", V((n_l, n_px, ch), BF16)), ("wo_g", V((n_l, nt, ch, dm), BF16)), ("wi_g", V((2, nt, dm, ch), BF16)),
                    ("stat", V((rows_all // 128, 128), F32)),
                    ("stat_rx", V((nt - 1, rows_all // 128, 128), F32)), ("h0", V((rows_all, dm), BF16)),
@@ -509,10 +551,10 @@
                    ("sums", V((nj // 2, nt, rj, dm), F32)), ("rxs", V((n_l, 6, nt // 2, rj, dm), BF16)),
                    ("tx2s", V((n_l, 2, nt // 2, rj, dm), BF16)), ("delta", V((nt, rj, dm), F32)),
                    ("hg", V((nj, nt, rj, dm), BF16)), ("fin", V((nj, nt, rj, dm), BF16)), ("dst", V((nt, rj, dm), BF16)),
-                   ("send_sem", pltpu.SemaphoreType.DMA((120,))), ("recv_sem", pltpu.SemaphoreType.DMA((120,))),
-                   ("loc_sem", pltpu.SemaphoreType.DMA((32,)))]
+                   ("send_sem", pltpu.SemaphoreType.DMA((3,))), ("small_sem", pltpu.SemaphoreType.DMA((6,))),
+                   ("recv_sem", pltpu.SemaphoreType.DMA((104,))), ("loc_sem", pltpu.SemaphoreType.DMA((22,)))]
         names = [n for n, *_ in ins] + [n for n, _ in outs] + [n for n, _ in scratch]
-        r_new, conv_new, ssm_new = pl.pallas_call(
+        held = pl.pallas_call(
             functools.partial(mixer_kernel, names, nt, nj, n_state),
             out_shape=[s for _, s in outs],
             in_specs=[s for _, _, s in ins],
@@ -522,6 +564,15 @@
             name="mixer",
         )(*[a for _, a, _ in ins])
 
+        r_new, conv_new, ssm_new = pl.pallas_call(
+            flush_kernel,
+            out_shape=[jax.ShapeDtypeStruct(a.shape, a.dtype) for a in held],
+            in_specs=[pl.BlockSpec(memory_space=V)] * 3,
+            out_specs=[hb] * 3,
+            scratch_shapes=[pltpu.SemaphoreType.DMA((3,))],
+            compiler_params=pltpu.CompilerParams(vmem_limit_bytes=2**20),
+            name="flush",
+        )(*[pltpu.with_memory_space_constraint(a, V) for a in held])
         return r_new, jnp.transpose(conv_new, (0, 2, 3, 1)), jnp.transpose(ssm_new, (0, 1, 3, 2))
 
     cache_spec = P(None, ("dp", "tx"), "ty", None)

time: 103 us -> 96.4 us (0.936)
  local copies, waits for them, and re-layouts: 9.37 us -> 0 us
  Pallas kernels: 93.1 us -> 95.7 us
    unnamed x4 -> x0, local copies, waits for them, and re-layouts: 9.37 us -> none
    pallas_call x0 -> x1, Pallas kernels: none -> 5.71 us  [local_step(): pl.pallas_call(flush_kernel, out_shape=[jax.ShapeDtypeStruct(a.shape, a.d...]
    pallas_call x1, Pallas kernels: 93.1 us -> 89.9 us  [local_step(): pl.pallas_call(functools.partial(mixer_kernel, names, nt, nj, n_state), o...]
where the time goes in v3:
time: 96.4 us; the launch traced here: 96.3 us
  Pallas kernels  95.7 us (99%)
    pallas_call x1, Pallas kernels, local_step(): pl.pallas_call(functools.partial(mixer_kernel, names, nt, nj, n_state), o...  89.9 us
    pallas_call x1, Pallas kernels, local_step(): pl.pallas_call(flush_kernel, out_shape=[jax.ShapeDtypeStruct(a.shape, a.d...  5.71 us

profile of v3, /device:TPU:97, one launch (start us, length us, event | category | flops | bytes accessed | tf_op | source)
XLA Modules:
  0.0 96.3 jit_solution(8614135380609358265)
XLA Ops:
  0.6 89.9 %mixer.1 = (f32[1024,384]{1,0:T(8,128)S(1)}, bf16[2,3,256,384]{3,2,1,0:T(8,128)(2,1)S(1)}, f32[2,256,16,384]{3,2,1,0:T(8,128)S(1)}) custom-call(f32[1024,384]{1,0:T(8,128)} %refs_0_.1, f32[2,384]{1,0:T(2,128)} %refs_1_.1, f32[2,4,384]{2,1,0:T(4,128)} %bitcast.9, f32[2,384]{1,0:T(2,128)} %refs_3_.1, f32[2,384]{1,0:T(2,128)} %refs_4_.1, f32[2,384]{1,0:T(2,128)} %refs_5_.1, ...), custom_call_target="tpu_custom_call" | custom-call | tf_op jit(solution)/shard_map/mixer/pallas_call | solution.py:557
  90.6 5.7 %flush.1 = (f32[1024,384]{1,0:T(8,128)}, bf16[2,3,256,384]{3,2,1,0:T(8,128)(2,1)}, f32[2,256,16,384]{3,2,1,0:T(8,128)}) custom-call(f32[1024,384]{1,0:T(8,128)S(1)} %get-tuple-element.9.refs_0_, bf16[2,3,256,384]{3,2,1,0:T(8,128)(2,1)S(1)} %get-tuple-element.10.refs_1_, f32[2,256,16,384]{3,2,1,0:T(8,128)S(1)} %get-tuple-element.11.refs_2_), custom_call_target="tpu_custom_call" | custom-call | tf_op jit(solution)/shard_map/flush/pallas_call | solution.py:567
